TPU v7x, 256 devices: a whole 4x4x8 slice. The times are simulated.
256 devices in a mesh: row: 16 (over y, x_hi, core), col: 16 (over x_lo, z).
Axes of the slice: x: 4 (x_hi: 2, x_lo: 2; x = x_hi * 2 + x_lo), y: 4, z: 8, core: 2. Of those that a mesh axis runs over, the one named last changes fastest.
Arguments:
- grad_out: bfloat16 [512, 512, 320], P('row', 'col'), may hold values from -0.0390625 to 0.0390625
- dec_pre: bfloat16 [512, 512, 320], P('row', 'col'), may hold values from -6 to 6
- ctrl_out: bfloat16 [512, 512, 320], P('row', 'col'), may hold values from -6 to 6
- ctrl_mid: bfloat16 [512, 512, 320], P('row', 'col'), may hold values from -6 to 6
- ctrl_in: bfloat16 [512, 512, 320], P('row', 'col'), may hold values from -6 to 6
- dec_weight: bfloat16 [3, 3, 320, 320], replicated, may hold values from -0.109375 to 0.109375
- zero_weight: bfloat16 [320, 320], replicated, may hold values from -0.3125 to 0.3125
- ctrl_weight: bfloat16 [3, 3, 320, 320], replicated, may hold values from -0.109375 to 0.109375
Outputs:
- grad_zero: float32 [320, 320], P('row', 'col')
- grad_ctrl: float32 [3, 3, 320, 320], P(None, None, 'row', 'col')
- grad_in: float32 [3, 3, 320, 320], P(None, None, 'row', 'col')
All inputs are finite; a program needn't handle non-finite values.
Results may differ from a plain program's by a relative error of at most 0.024.
Values may be sent and summed in bfloat16 or wider, within the bound.
A program may use at most 128 MiB of HBM per device.

v0:
```python
import jax
import jax.numpy as jnp
from jax import lax
from jax.sharding import PartitionSpec as P


def with_halo(cells, sides, width):
    for axis, dim in sides:
        count = lax.axis_size(axis)
        ends = count - 1
        head = lax.slice_in_dim(cells, 0, width, axis=dim)
        tail = lax.slice_in_dim(cells, cells.shape[dim] - width, cells.shape[dim], axis=dim)
        cells = jnp.concatenate(
            [
                lax.ppermute(tail, axis, [(i, (i + 1) % count) for i in range(ends)]),
                cells,
                lax.ppermute(head, axis, [((i + 1) % count, i) for i in range(ends)]),
            ],
            axis=dim,
        )
    return cells


def in_blocks(array, dim, devices):
    lengths = array.shape
    blocks = array.reshape(*lengths[:dim], devices, lengths[dim] // devices, *lengths[dim + 1 :])
    return jnp.moveaxis(blocks, dim, 0)


def sent_and_summed(array, axis, dim):
    blocks = in_blocks(array, dim, lax.axis_size(axis))
    arrived = lax.all_to_all(blocks, axis, split_axis=0, concat_axis=0, tiled=True)
    return arrived.sum(axis=0)


def silu_slope(values):
    sigm = jax.nn.sigmoid(values)
    return sigm * (1.0 + values * (1.0 - sigm))


def transpose_local(padded, kernel, height, breadth):
    channels = padded.shape[2]
    summed = jnp.zeros((height * breadth, kernel.shape[2]), jnp.float32)
    for tap_row in range(3):
        for tap_col in range(3):
            window = padded[
                2 - tap_row : 2 - tap_row + height, 2 - tap_col : 2 - tap_col + breadth
            ].reshape(-1, channels)
            summed = summed + lax.dot_general(
                window,
                kernel[tap_row, tap_col],
                (((1,), (1,)), ((), ())),
                preferred_element_type=jnp.float32,
            )
    return summed.reshape(height, breadth, -1)


def weight_local(padded, cotangent):
    height, breadth, channels = cotangent.shape
    flat_grad = cotangent.reshape(-1, channels)
    taps = []
    for tap_row in range(3):
        for tap_col in range(3):
            window = padded[tap_row : tap_row + height, tap_col : tap_col + breadth].reshape(
                -1, padded.shape[2]
            )
            taps.append(
                lax.dot_general(
                    window, flat_grad, (((0,), (0,)), ((), ())), preferred_element_type=jnp.float32
                )
            )
    return jnp.stack(taps)


def on_device(grad_out, dec_pre, ctrl_out, ctrl_mid, ctrl_in, dec_weight, zero_weight, ctrl_weight):
    height, breadth, channels = grad_out.shape
    grad_pad = with_halo(grad_out, (("row", 0), ("col", 1)), 1)
    activations = jnp.concatenate(
        [jax.nn.silu(ctrl_mid.astype(jnp.float32)), jax.nn.silu(ctrl_in.astype(jnp.float32))],
        axis=2,
    ).astype(jnp.bfloat16)
    act_pad = with_halo(activations, (("row", 0), ("col", 1)), 1)
    dec_grad = (
        silu_slope(dec_pre.astype(jnp.float32))
        * transpose_local(grad_pad, dec_weight, height, breadth)
    ).astype(jnp.bfloat16)
    flat_dec = dec_grad.reshape(-1, channels)
    zero_part = lax.dot_general(
        ctrl_out.reshape(-1, channels),
        flat_dec,
        (((0,), (0,)), ((), ())),
        preferred_element_type=jnp.float32,
    )
    ctrl_grad = (
        lax.dot_general(
            flat_dec, zero_weight, (((1,), (1,)), ((), ())), preferred_element_type=jnp.float32
        )
        .astype(jnp.bfloat16)
        .reshape(height, breadth, channels)
    )
    ctrl_pad = with_halo(ctrl_grad, (("row", 0), ("col", 1)), 1)
    mid_grad = (
        silu_slope(ctrl_mid.astype(jnp.float32))
        * transpose_local(ctrl_pad, ctrl_weight, height, breadth)
    ).astype(jnp.bfloat16)
    ctrl_part = weight_local(act_pad[:, :, :channels], ctrl_grad)
    input_part = weight_local(act_pad[:, :, channels:], mid_grad)
    stacked = jnp.concatenate([zero_part[None], ctrl_part, input_part], axis=0)
    reduced = lax.psum_scatter(
        stacked.astype(jnp.bfloat16), "row", scatter_dimension=1, tiled=True
    ).astype(jnp.float32)
    reduced = sent_and_summed(reduced, "col", 2)
    rows_own = reduced.shape[1]
    cols_own = reduced.shape[2]
    grad_zero = reduced[0]
    grad_ctrl = reduced[1:10].reshape(3, 3, rows_own, cols_own)
    grad_in = reduced[10:19].reshape(3, 3, rows_own, cols_own)
    return (grad_zero, grad_ctrl, grad_in)


def solution(mesh):
    in_specs = (
        P("row", "col", None),
        P("row", "col", None),
        P("row", "col", None),
        P("row", "col", None),
        P("row", "col", None),
        P(),
        P(),
        P(),
    )
    out_specs = (P("row", "col"), P(None, None, "row", "col"), P(None, None, "row", "col"))
    return jax.shard_map(
        on_device, mesh=mesh, in_specs=in_specs, out_specs=out_specs, check_vma=False
    )
```

profile of v0, /device:TPU:1, one launch (start us, length us, event | category | flops | bytes accessed | tf_op | source)
XLA Modules:
  0.0 279.3 jit_solution(9337680217182300094)
XLA Ops:
  8.1 6.0 %collective-permute-start = (bf16[1,32,320]{2,1,0:T(8,128)(2,1)S(1)}, bf16[1,32,320]{2,1,0:T(8,128)(2,1)S(1)}, u32[]{:S(2)}, u32[]{:S(2)}) collective-permute-start(bf16[1,32,320]{2,1,0:T(8,128)(2,1)S(1)} %get-tuple-element.46), channel_id=1, source_target_pairs={{0,16},{16,32},{32,48},{48,64},{64,80},{80,96},{96,112},{112,128},... | collective-permute-start | bytes 61448 | tf_op jit(solution)/shard_map/ppermute | solution.py:15
  14.1 1.9 collective-permute-start.1
  16.0 4.7 %collective-permute-done.1 = bf16[1,32,320]{2,1,0:T(8,128)(2,1)S(1)} collective-permute-done((bf16[1,32,320]{2,1,0:T(8,128)(2,1)S(1)}, bf16[1,32,320]{2,1,0:T(8,128)(2,1)S(1)}, u32[]{:S(2)}, u32[]{:S(2)}) %collective-permute-start.1) | collective-permute-done | bytes 20512 | tf_op jit(solution)/shard_map/ppermute | solution.py:17
  20.7 2.0 pad_maximum_fusion.8
  24.1 4.2 %collective-permute-start.3 = (bf16[34,1,320]{2,1,0:T(2,128)(2,1)S(1)}, bf16[34,1,320]{2,1,0:T(2,128)(2,1)S(1)}, u32[]{:S(2)}, u32[]{:S(2)}) collective-permute-start(bf16[34,1,320]{2,1,0:T(2,128)(2,1)S(1)} %get-tuple-element.37), channel_id=1, source_target_pairs={{0,1},{1,2},{2,3},{3,4},{4,5},{5,6},{6,7},{7,8},{8,9},{9,10},{10,1... | collective-permute-start | bytes 65288 | tf_op jit(solution)/shard_map/ppermute | solution.py:15
  29.5 3.0 %pad_maximum_fusion.7 = (bf16[32,32,320]{2,1,0:T(8,128)(2,1)S(1)}, bf16[32,32,320]{2,1,0:T(8,128)(2,1)S(1)}, bf16[32,32,320]{2,1,0:T(8,128)(2,1)S(1)}, bf16[32,3...) fusion(bf16[34,1,320]{2,1,0:T(2,128)(2,1)S(1)} %collective-permute-done.2, ...), kind=kLoop, calls=%fused_computation.140 | loop fusion | flops 7864320 | bytes 4672000 | tf_op jit(solution)/shard_map/concatenate | solution.py:13
  42.4 2.9 %collective-permute-start.8 = (bf16[1,32,320]{1,2,0:T(8,128)(2,1)S(1)}, bf16[1,32,320]{1,2,0:T(8,128)(2,1)S(1)}, u32[]{:S(2)}, u32[]{:S(2)}) collective-permute-start(bf16[1,32,320]{1,2,0:T(8,128)(2,1)S(1)} %get-tuple-element.47), channel_id=1, source_target_pairs={{0,16},{16,32},{32,48},{48,64},{64,80},{80,96},{96,112},{112,128},... | collective-permute-start | bytes 61448 | tf_op jit(solution)/shard_map/ppermute | solution.py:15
  48.1 4.4 %collective-permute-done.9 = bf16[1,32,320]{1,2,0:T(8,128)(2,1)S(1)} collective-permute-done((bf16[1,32,320]{1,2,0:T(8,128)(2,1)S(1)}, bf16[1,32,320]{1,2,0:T(8,128)(2,1)S(1)}, u32[]{:S(2)}, u32[]{:S(2)}) %collective-permute-start.9) | collective-permute-done | bytes 20512 | tf_op jit(solution)/shard_map/ppermute | solution.py:17
  54.4 4.8 %collective-permute-start.11 = (bf16[34,1,320]{2,1,0:T(2,128)(2,1)S(1)}, bf16[34,1,320]{2,1,0:T(2,128)(2,1)S(1)}, u32[]{:S(2)}, u32[]{:S(2)}) collective-permute-start(bf16[34,1,320]{2,1,0:T(2,128)(2,1)S(1)} %get-tuple-element.31), channel_id=1, source_target_pairs={{0,1},{1,2},{2,3},{3,4},{4,5},{5,6},{6,7},{7,8},{8,9},{9,10},{10,1... | collective-permute-start | bytes 65288 | tf_op jit(solution)/shard_map/ppermute | solution.py:15
  67.3 2.4 fusion.18
  69.8 2.7 collective-permute-start.4
  72.5 1.9 collective-permute-start.5
  75.7 3.6 %collective-permute-done.5 = bf16[1,32,640]{2,1,0:T(8,128)(2,1)S(1)} collective-permute-done((bf16[1,32,640]{2,1,0:T(8,128)(2,1)S(1)}, bf16[1,32,640]{2,1,0:T(8,128)(2,1)S(1)}, u32[]{:S(2)}, u32[]{:S(2)}) %collective-permute-start.5) | collective-permute-done | bytes 40992 | tf_op jit(solution)/shard_map/ppermute | solution.py:17
  79.6 4.0 %collective-permute-start.6 = (bf16[34,1,640]{2,1,0:T(2,128)(2,1)S(1)}, bf16[34,1,640]{2,1,0:T(2,128)(2,1)S(1)}, u32[]{:S(2)}, u32[]{:S(2)}) collective-permute-start(bf16[34,1,640]{2,1,0:T(2,128)(2,1)S(1)} %get-tuple-element.12), channel_id=1, source_target_pairs={{0,1},{1,2},{2,3},{3,4},{4,5},{5,6},{6,7},{7,8},{8,9},{9,10},{10,1... | collective-permute-start | bytes 130568 | tf_op jit(solution)/shard_map/ppermute | solution.py:15
  85.7 3.7 %collective-permute-done.7 = bf16[34,1,640]{2,1,0:T(2,128)(2,1)S(1)} collective-permute-done((bf16[34,1,640]{2,1,0:T(2,128)(2,1)S(1)}, bf16[34,1,640]{2,1,0:T(2,128)(2,1)S(1)}, u32[]{:S(2)}, u32[]{:S(2)}) %collective-permute-start.7) | collective-permute-done | bytes 43552 | tf_op jit(solution)/shard_map/ppermute | solution.py:17
  89.4 3.2 %pad_maximum_fusion = (bf16[34,33,640]{2,1,0:T(8,128)(2,1)S(1)}, bf16[34,33,640]{2,1,0:T(8,128)(2,1)S(1)}) fusion(bf16[34,1,640]{2,1,0:T(2,128)(2,1)S(1)} %collective-permute-done.7, bf16[1,32,640]{2,1,0:T(8,128)(2,1)S(1)} %collective-permute-done.5, bf16[32,32,320]{2,1,0:T(8,128)(2,1)S(1)} %fusion.10, bf16[32,32,320]{2,1,0:T(8,128)(2,1)S(1)} %get-tuple-element.39, ...), kind=kLoop, calls=%fused_computation.8 | loop fusion | flops 14361600 | bytes 4352000 | tf_op jit(solution)/shard_map/concatenate | solution.py:13
  117.5 8.9 %copy.114 = bf16[19,320,320]{2,0,1:T(8,128)(2,1)} copy(bf16[19,320,320]{1,2,0:T(8,128)(2,1)} %fusion.34) | data formatting | bytes 7782400 | tf_op jit(solution)/shard_map/concatenate | solution.py:108
  126.4 105.3 %reduce-scatter.2.cloned.1.call-done = bf16[19,20,320]{2,0,1:T(8,128)(2,1)} async-done(((bf16[19,320,320]{2,0,1:T(8,128)(2,1)}), bf16[19,20,320]{2,0,1:T(8,128)(2,1)}) %reduce-scatter.2.cloned.1.call-update) | async-done | bytes 243216 | tf_op jit(solution)/shard_map/reduce_scatter | solution.py:109
  232.8 3.6 %reshape.152 = f32[19,20,16,20]{3,2,1,0:T(8,128)} reshape(f32[19,20,320]{2,1,0:T(8,128)S(1)} %copy_convert_fusion) | data formatting | bytes 972800 | tf_op jit(solution)/shard_map/transpose | solution.py:27
  236.4 4.7 %copy.116 = f32[16,19,20,20]{3,2,1,0:T(8,128)} copy(f32[16,19,20,20]{3,0,2,1:T(8,128)} %bitcast.304) | data formatting | bytes 972800 | tf_op jit(solution)/shard_map/transpose | solution.py:27
  241.1 3.6 %reshape.163 = f32[16,1,7600]{2,1,0:T(1,128)S(1)} reshape(f32[16,19,20,20]{3,2,1,0:T(8,128)} %copy.116) | data formatting | bytes 972800
  244.7 18.9 %all_to_all.5 = f32[16,1,7600]{2,1,0:T(1,128)S(1)} all-to-all(f32[16,1,7600]{2,1,0:T(1,128)S(1)} %reshape.163), channel_id=1, replica_groups=mesh['row'=16,'col'=16] {'col'}, dimensions={0} | all-to-all | bytes 972800 | tf_op jit(solution)/shard_map/all_to_all | solution.py:32
  265.9 2.9 %reshape.164 = f32[16,19,20,20]{3,2,1,0:T(8,128)} reshape(f32[16,7600]{1,0:T(8,128)S(1)} %reduce) | data formatting | bytes 972800
  268.8 2.4 reduce_sum.9
  (100 shorter events, 59.0 us)
Async XLA Ops:
  7.2 67.3 %copy-start = (bf16[32,32,320]{2,1,0:T(8,128)(2,1)S(1)}, bf16[32,32,320]{2,1,0:T(8,128)(2,1)}, u32[]{:S(2)}) copy-start(bf16[32,32,320]{2,1,0:T(8,128)(2,1)} %param.10) | copy-start | bytes 1966084
  7.2 224.6 %reduce-scatter.2.cloned.1.call-start = ((), (), s32[]{:S(2)}) async-start(), calls=%async_computation.2 | async-start | bytes 6266880 | tf_op jit(solution)/shard_map/reduce_scatter | solution.py:109
  8.1 8.0 %collective-permute-start = (bf16[1,32,320]{2,1,0:T(8,128)(2,1)S(1)}, bf16[1,32,320]{2,1,0:T(8,128)(2,1)S(1)}, u32[]{:S(2)}, u32[]{:S(2)}) collective-permute-start(bf16[1,32,320]{2,1,0:T(8,128)(2,1)S(1)} %get-tuple-element.46), channel_id=1, source_target_pairs={{0,16},{16,32},{32,48},{48,64},{64,80},{80,96},{96,112},{112,128},... | collective-permute-start | bytes 61448 | tf_op jit(solution)/shard_map/ppermute | solution.py:15
  14.1 6.7 %collective-permute-start.1 = (bf16[1,32,320]{2,1,0:T(8,128)(2,1)S(1)}, bf16[1,32,320]{2,1,0:T(8,128)(2,1)S(1)}, u32[]{:S(2)}, u32[]{:S(2)}) collective-permute-start(bf16[1,32,320]{2,1,0:T(8,128)(2,1)S(1)} %get-tuple-element.45), channel_id=1, source_target_pairs={{16,0},{32,16},{48,32},{64,48},{80,64},{96,80},{112,96},{128,112},... | collective-permute-start | bytes 61448 | tf_op jit(solution)/shard_map/ppermute | solution.py:17
  16.0 12.3 %copy-start.6 = (bf16[3,3,320,320]{3,2,1,0:T(8,128)(2,1)S(1)}, bf16[3,3,320,320]{3,2,1,0:T(8,128)(2,1)}, u32[]{:S(2)}) copy-start(bf16[3,3,320,320]{3,2,1,0:T(8,128)(2,1)} %param.13) | copy-start | bytes 5529604
  22.8 6.6 %collective-permute-start.2 = (bf16[34,1,320]{2,1,0:T(2,128)(2,1)S(1)}, bf16[34,1,320]{2,1,0:T(2,128)(2,1)S(1)}, u32[]{:S(2)}, u32[]{:S(2)}) collective-permute-start(bf16[34,1,320]{2,1,0:T(2,128)(2,1)S(1)} %get-tuple-element.36), channel_id=1, source_target_pairs={{1,0},{2,1},{3,2},{4,3},{5,4},{6,5},{7,6},{8,7},{9,8},{10,9},{11,1... | collective-permute-start | bytes 65288 | tf_op jit(solution)/shard_map/ppermute | solution.py:17
  24.1 5.4 %collective-permute-start.3 = (bf16[34,1,320]{2,1,0:T(2,128)(2,1)S(1)}, bf16[34,1,320]{2,1,0:T(2,128)(2,1)S(1)}, u32[]{:S(2)}, u32[]{:S(2)}) collective-permute-start(bf16[34,1,320]{2,1,0:T(2,128)(2,1)S(1)} %get-tuple-element.37), channel_id=1, source_target_pairs={{0,1},{1,2},{2,3},{3,4},{4,5},{5,6},{6,7},{7,8},{8,9},{9,10},{10,1... | collective-permute-start | bytes 65288 | tf_op jit(solution)/shard_map/ppermute | solution.py:15
  34.2 1.1 copy-start.2
  39.9 1.8 copy-start.9
  41.7 5.5 %copy-start.3 = (bf16[32,32,320]{2,1,0:T(8,128)(2,1)}, bf16[32,32,320]{2,1,0:T(8,128)(2,1)S(1)}, u32[]{:S(2)}) copy-start(bf16[32,32,320]{2,1,0:T(8,128)(2,1)S(1)} %fusion.6) | copy-start | bytes 1966084
  41.7 5.5 %copy-start.7 = (bf16[32,32,320]{2,1,0:T(8,128)(2,1)S(1)}, bf16[32,32,320]{2,1,0:T(8,128)(2,1)}, u32[]{:S(2)}) copy-start(bf16[32,32,320]{2,1,0:T(8,128)(2,1)} %param.12) | copy-start | bytes 1966084
  42.4 5.6 %collective-permute-start.8 = (bf16[1,32,320]{1,2,0:T(8,128)(2,1)S(1)}, bf16[1,32,320]{1,2,0:T(8,128)(2,1)S(1)}, u32[]{:S(2)}, u32[]{:S(2)}) collective-permute-start(bf16[1,32,320]{1,2,0:T(8,128)(2,1)S(1)} %get-tuple-element.47), channel_id=1, source_target_pairs={{0,16},{16,32},{32,48},{48,64},{64,80},{80,96},{96,112},{112,128},... | collective-permute-start | bytes 61448 | tf_op jit(solution)/shard_map/ppermute | solution.py:15
  45.2 7.3 %collective-permute-start.9 = (bf16[1,32,320]{1,2,0:T(8,128)(2,1)S(1)}, bf16[1,32,320]{1,2,0:T(8,128)(2,1)S(1)}, u32[]{:S(2)}, u32[]{:S(2)}) collective-permute-start(bf16[1,32,320]{1,2,0:T(8,128)(2,1)S(1)} %get-tuple-element.48), channel_id=1, source_target_pairs={{16,0},{32,16},{48,32},{64,48},{80,64},{96,80},{112,96},{128,112},... | collective-permute-start | bytes 61448 | tf_op jit(solution)/shard_map/ppermute | solution.py:17
  52.6 6.6 %copy-start.5 = (bf16[3,3,320,320]{3,2,1,0:T(8,128)(2,1)S(1)}, bf16[3,3,320,320]{3,2,1,0:T(8,128)(2,1)}, u32[]{:S(2)}) copy-start(bf16[3,3,320,320]{3,2,1,0:T(8,128)(2,1)} %param.15) | copy-start | bytes 5529604
  52.9 6.8 %collective-permute-start.10 = (bf16[34,1,320]{2,1,0:T(2,128)(2,1)S(1)}, bf16[34,1,320]{2,1,0:T(2,128)(2,1)S(1)}, u32[]{:S(2)}, u32[]{:S(2)}) collective-permute-start(bf16[34,1,320]{2,1,0:T(2,128)(2,1)S(1)} %get-tuple-element.32), channel_id=1, source_target_pairs={{1,0},{2,1},{3,2},{4,3},{5,4},{6,5},{7,6},{8,7},{9,8},{10,9},{11,1... | collective-permute-start | bytes 65288 | tf_op jit(solution)/shard_map/ppermute | solution.py:17
  54.4 5.8 %collective-permute-start.11 = (bf16[34,1,320]{2,1,0:T(2,128)(2,1)S(1)}, bf16[34,1,320]{2,1,0:T(2,128)(2,1)S(1)}, u32[]{:S(2)}, u32[]{:S(2)}) collective-permute-start(bf16[34,1,320]{2,1,0:T(2,128)(2,1)S(1)} %get-tuple-element.31), channel_id=1, source_target_pairs={{0,1},{1,2},{2,3},{3,4},{4,5},{5,6},{6,7},{7,8},{8,9},{9,10},{10,1... | collective-permute-start | bytes 65288 | tf_op jit(solution)/shard_map/ppermute | solution.py:15
  67.3 7.1 %copy-start.4 = (bf16[32,32,320]{2,1,0:T(8,128)(2,1)S(1)}, bf16[32,32,320]{2,1,0:T(8,128)(2,1)}, u32[]{:S(2)}) copy-start(bf16[32,32,320]{2,1,0:T(8,128)(2,1)} %copy-done.3) | copy-start | bytes 1966084
  69.8 5.9 %collective-permute-start.4 = (bf16[1,32,640]{2,1,0:T(8,128)(2,1)S(1)}, bf16[1,32,640]{2,1,0:T(8,128)(2,1)S(1)}, u32[]{:S(2)}, u32[]{:S(2)}) collective-permute-start(bf16[1,32,640]{2,1,0:T(8,128)(2,1)S(1)} %get-tuple-element.15), channel_id=1, source_target_pairs={{0,16},{16,32},{32,48},{48,64},{64,80},{80,96},{96,112},{112,128},... | collective-permute-start | bytes 122888 | tf_op jit(solution)/shard_map/ppermute | solution.py:15
  72.5 6.8 %collective-permute-start.5 = (bf16[1,32,640]{2,1,0:T(8,128)(2,1)S(1)}, bf16[1,32,640]{2,1,0:T(8,128)(2,1)S(1)}, u32[]{:S(2)}, u32[]{:S(2)}) collective-permute-start(bf16[1,32,640]{2,1,0:T(8,128)(2,1)S(1)} %get-tuple-element.16), channel_id=1, source_target_pairs={{16,0},{32,16},{48,32},{64,48},{80,64},{96,80},{112,96},{128,112},... | collective-permute-start | bytes 122888 | tf_op jit(solution)/shard_map/ppermute | solution.py:17
  79.6 6.1 %collective-permute-start.6 = (bf16[34,1,640]{2,1,0:T(2,128)(2,1)S(1)}, bf16[34,1,640]{2,1,0:T(2,128)(2,1)S(1)}, u32[]{:S(2)}, u32[]{:S(2)}) collective-permute-start(bf16[34,1,640]{2,1,0:T(2,128)(2,1)S(1)} %get-tuple-element.12), channel_id=1, source_target_pairs={{0,1},{1,2},{2,3},{3,4},{4,5},{5,6},{6,7},{7,8},{8,9},{9,10},{10,1... | collective-permute-start | bytes 130568 | tf_op jit(solution)/shard_map/ppermute | solution.py:15
  83.6 5.8 %collective-permute-start.7 = (bf16[34,1,640]{2,1,0:T(2,128)(2,1)S(1)}, bf16[34,1,640]{2,1,0:T(2,128)(2,1)S(1)}, u32[]{:S(2)}, u32[]{:S(2)}) collective-permute-start(bf16[34,1,640]{2,1,0:T(2,128)(2,1)S(1)} %get-tuple-element.11), channel_id=1, source_target_pairs={{1,0},{2,1},{3,2},{4,3},{5,4},{6,5},{7,6},{8,7},{9,8},{10,9},{11,1... | collective-permute-start | bytes 130568 | tf_op jit(solution)/shard_map/ppermute | solution.py:17
  108.6 1.5 copy-start.8
  265.9 6.6 %copy-start.1 = (bf16[32,32,320]{2,1,0:T(8,128)(2,1)S(1)}, bf16[32,32,320]{2,1,0:T(8,128)(2,1)}, u32[]{:S(2)}) copy-start(bf16[32,32,320]{2,1,0:T(8,128)(2,1)} %param.10) | copy-start | bytes 1966084
Sparse Core Ops, SparseCore 0:
  126.5 105.1 reduce-scatter.1
where the time goes:
time: 282 us; the launch traced here: 279 us
  waiting for transfers between devices  122 us (43%)
  matrix products  36.8 us (13%)
  starting transfers between devices  34.3 us (12%)
  local copies, waits for them, and re-layouts  32.5 us (12%)
  other arithmetic  19.9 us (7%)
  blocking collectives  18.9 us (7%)
  between operations  14.6 us (5%)
    reduce_scatter x1, waiting for transfers between devices, on_device(): lax.psum_scatter(stacked.astype(jnp.bfloat16), 'row', scatter_dimension=1...  105 us
    ppermute x6, starting transfers between devices, with_halo(): lax.ppermute(tail, axis, [(i, (i + 1) % count) for i in range(ends)])  24.5 us
    dot_general x18, matrix products, weight_local(): lax.dot_general(window, flat_grad, (((0,), (0,)), ((), ())), preferred_el...  24.2 us
    all_to_all x1, blocking collectives, sent_and_summed(): lax.all_to_all(blocks, axis, split_axis=0, concat_axis=0, tiled=True)  18.9 us
    ppermute x6, waiting for transfers between devices, with_halo(): lax.ppermute(head, axis, [((i + 1) % count, i) for i in range(ends)])  16.4 us
    dot_general x18, matrix products, transpose_local(): lax.dot_general(window, kernel[tap_row, tap_col], (((1,), (1,)), ((), ())...  10.8 us
    concatenate x8, other arithmetic, with_halo(): jnp.concatenate([lax.ppermute(tail, axis, [(i, (i + 1) % count) for i in...  9.99 us
    ppermute x6, starting transfers between devices, with_halo(): lax.ppermute(head, axis, [((i + 1) % count, i) for i in range(ends)])  9.77 us
  transfers between devices with their start and end apart: 13, of which 7 were waited for; matrix products, arithmetic and copies ran while one was open for 2% of the time, Pallas kernels for 0%

commit v1 on v0

v1 whole, which is shorter than its diff:
```python
import functools

import jax
import jax.numpy as jnp
import numpy as np
from jax import lax
from jax.experimental import pallas as pl
from jax.experimental.pallas import tpu as pltpu
from jax.sharding import PartitionSpec as P

F32 = jnp.float32
BF16 = jnp.bfloat16
MESH = pl.DeviceIdType.MESH
NT = (((1,), (1,)), ((), ()))
NN = (((1,), (0,)), ((), ()))
C = 320
T = 32
ROWS_A, SPLIT_A, ZA = 320, 160, 48
ROWS_B, SPLIT_B, ZB = 240, 128, 32


def dot(a, b, dims=NN):
    return lax.dot_general(a, b, dims, preferred_element_type=F32)


def silu(v):
    return v * jax.nn.sigmoid(v)


def slope(v):
    s = jax.nn.sigmoid(v)
    return s * (1.0 + v * (1.0 - s))


def tables():
    place = np.full((16, 256), -1, np.int32)
    for y in range(4):
        for s in range(3):
            for xh in range(2):
                for core in range(2):
                    for c in range(20):
                        lane = xh * 128 + core * 64 + s * 20 + c
                        place[y * 3 + s, lane] = y * 80 + xh * 40 + core * 20 + c - (128 if y == 3 else 0)
    order = np.zeros((C, 1), np.int32)
    for core in range(2):
        for xl in range(2):
            for z in range(8):
                for i in range(10):
                    order[core * 160 + xl * 80 + z * 10 + i, 0] = (xl * 8 + z) * 20 + core * 10 + i
    za = np.full((8 * ZA, 1), -1, np.int32)
    zb = np.full((8 * ZB, 1), -1, np.int32)
    for z in range(8):
        for g in range(4):
            for i in range(10):
                za[z * ZA + g * 10 + i, 0] = g * 80 + z * 10 + i
                if g < 3:
                    zb[z * ZB + g * 10 + i, 0] = g * 80 + z * 10 + i
    return place, order, za, zb


def kernel(
    g_hbm, pre_hbm, cout_hbm, mid_hbm, cin_hbm, wd_hbm, wz_hbm, wc_hbm,
    place_ref, order_ref, za_ref, zb_ref,
    out_a, out_b,
    in4, pre, cout, wd, wz, wc,
    scol, hrow, hcol, hcor, hc32,
    sh, rem, wrem, dec, xmid, xin, xout, pmat, omat, gt, mgrad,
    ra, ca, ya, xa, ea, fa, ya2, xa2, da, zsa, zra, fina, pina,
    rb, cb, yb, xb, eb, fb, yb2, xb2, db, zsb, zrb, finb, pinb,
    load_sem, hs_sem, hr_sem, cs_sem, cr_sem, ss_sem, sr_sem,
):
    row = lax.axis_index("row")
    col = lax.axis_index("col")
    y, xh, core = row // 4, (row // 2) % 2, row % 2
    xl, z = col // 8, col % 8
    x = xh * 2 + xl

    def at_y(t):
        return ((t * 2 + xh) * 2 + core, col)

    def at_x(t):
        return ((y * 2 + t // 2) * 2 + core, (t % 2) * 8 + z)

    def at_z(t):
        return (row, xl * 8 + t)

    partner = (row + 1 - 2 * core, col)

    loads = [
        pltpu.make_async_copy(g_hbm, in4.at[0], load_sem.at[0]),
        pltpu.make_async_copy(mid_hbm, in4.at[1], load_sem.at[1]),
        pltpu.make_async_copy(cin_hbm, in4.at[2], load_sem.at[2]),
        pltpu.make_async_copy(wd_hbm, wd, load_sem.at[3]),
        pltpu.make_async_copy(pre_hbm, pre, load_sem.at[4]),
        pltpu.make_async_copy(wz_hbm, wz, load_sem.at[5]),
        pltpu.make_async_copy(cout_hbm, cout, load_sem.at[6]),
        pltpu.make_async_copy(wc_hbm, wc, load_sem.at[7]),
    ]
    for copy in loads:
        copy.start()

    has = {-1: (row > 0, col > 0), 1: (row < 15, col < 15), 0: (row >= 0, col >= 0)}
    around = [(dr, dc) for dr in (-1, 0, 1) for dc in (-1, 0, 1) if (dr, dc) != (0, 0)]
    there = {d: jnp.logical_and(has[d[0]][0], has[d[1]][1]) for d in around}

    barrier = pltpu.get_barrier_semaphore()
    for d in around:
        @pl.when(there[d])
        def _(d=d):
            pl.semaphore_signal(barrier, inc=1, device_id=(row + d[0], col + d[1]), device_id_type=MESH)
    peers = [partner]
    peers += [at_y((y + d) % 4) for d in range(1, 4)]
    peers += [at_x((x + d) % 4) for d in range(1, 4)]
    peers += [at_z((z + d) % 8) for d in range(1, 8)]
    for peer in peers:
        pl.semaphore_signal(barrier, inc=1, device_id=peer, device_id_type=MESH)

    lanes = lax.broadcasted_iota(jnp.int32, (256, 256), 0)
    for k in range(12):
        pmat[k] = jnp.where(lanes == place_ref[k : k + 1, :], 1.0, 0.0).astype(BF16)
    omat[...] = jnp.where(
        lax.broadcasted_iota(jnp.int32, (C, C), 1) == order_ref[...], 1.0, 0.0
    ).astype(BF16)

    for copy in loads[:3]:
        copy.wait()
    for k in range(3):
        scol[0, k] = in4[k, :, 0, :]
        scol[1, k] = in4[k, :, T - 1, :]

    count = jnp.int32(len(peers))
    for d in around:
        count = count + there[d].astype(jnp.int32)
    pl.semaphore_wait(barrier, count)

    def halo(first, size, phase):
        copies = []
        for n, (dr, dc) in enumerate(around):
            span = pl.ds(first, size)
            if dc == 0:
                src = in4.at[span, 0 if dr < 0 else T - 1]
                dst = hrow.at[1 if dr < 0 else 0, span]
            elif dr == 0:
                src = scol.at[0 if dc < 0 else 1, span]
                dst = hcol.at[1 if dc < 0 else 0, span]
            else:
                src = scol.at[0 if dc < 0 else 1, span, pl.ds(0 if dr < 0 else 16, 16)]
                dst = hcor.at[(1 if dr < 0 else 0) * 2 + (1 if dc < 0 else 0), span]
            copies.append(
                (
                    (dr, dc),
                    pltpu.make_async_remote_copy(
                        src_ref=src, dst_ref=dst,
                        send_sem=hs_sem.at[phase, n], recv_sem=hr_sem.at[phase, n],
                        device_id=(row + dr, col + dc), device_id_type=MESH,
                    ),
                )
            )
        return copies

    def start(copies):
        for d, copy in copies:
            pl.when(there[d])(copy.start)

    def landed(copies):
        for d, copy in copies:
            pl.when(there[(-d[0], -d[1])])(copy.wait_recv)

    first = halo(0, 3, 0)
    start(first)

    @pl.when(row == 0)
    def _():
        hrow[0] = jnp.zeros((4, T, C), BF16)
        hcor[0] = jnp.zeros((4, 16, C), BF16)
        hcor[1] = jnp.zeros((4, 16, C), BF16)

    @pl.when(row == 15)
    def _():
        hrow[1] = jnp.zeros((4, T, C), BF16)
        hcor[2] = jnp.zeros((4, 16, C), BF16)
        hcor[3] = jnp.zeros((4, 16, C), BF16)

    @pl.when(jnp.logical_and(col == 0, row > 0))
    def _():
        hcor[0] = jnp.zeros((4, 16, C), BF16)

    @pl.when(jnp.logical_and(col == 0, row < 15))
    def _():
        hcor[2] = jnp.zeros((4, 16, C), BF16)

    @pl.when(col == 0)
    def _():
        hcol[0] = jnp.zeros((4, T, C), BF16)

    @pl.when(jnp.logical_and(col == 15, row > 0))
    def _():
        hcor[1] = jnp.zeros((4, 16, C), BF16)

    @pl.when(jnp.logical_and(col == 15, row < 15))
    def _():
        hcor[3] = jnp.zeros((4, 16, C), BF16)

    @pl.when(col == 15)
    def _():
        hcol[1] = jnp.zeros((4, T, C), BF16)

    loads[3].wait()
    for a in range(3):
        for b in range(3):
            wrem[0, a, :, (2 - b) * 64 : (3 - b) * 64] = wd[a * 3 + b, :, 256:320]
        wrem[0, a, :, 192:256] = jnp.zeros((C, 64), BF16)

    edge = lax.broadcasted_iota(jnp.int32, (T, C), 0)

    def shifted(k, act, with_rem):
        for side in range(2):
            hc32[side, 0:1, :] = hcor[side, k].astype(F32)[15:16]
            hc32[side, 1:33, :] = hcol[side, k].astype(F32)
            hc32[side, 33:34, :] = hcor[2 + side, k].astype(F32)[0:1]

        def emit(i, cells):
            left = hc32[0, pl.ds(i, 1), :]
            right = hc32[1, pl.ds(i, 1), :]
            now = cells.astype(F32)
            if act:
                now, left, right = silu(now), silu(left), silu(right)
            minus = jnp.where(edge == 0, left, pltpu.roll(now, 1, 0))
            plus = jnp.where(edge == T - 1, right, pltpu.roll(now, T - 1, 0))
            for s, v in enumerate((minus, now, plus)):
                v = v.astype(BF16)
                sh[s, i] = v
                if with_rem:
                    rem[i, :, s * 64 : (s + 1) * 64] = v[:, 256:320]
            if with_rem:
                rem[i, :, 192:256] = jnp.zeros((T, 64), BF16)

        emit(0, hrow[0, k])
        emit(T + 1, hrow[1, k])

        @pl.loop(0, T)
        def _(i):
            emit(i + 1, in4[k, i])

    def conv(w, wr, i0):
        total = jnp.zeros((512, C), F32)
        for a in range(3):
            rows = pl.ds(i0 + 2 - a, 16)
            for s in range(3):
                total += dot(sh[s, rows].reshape(512, C)[:, :256], w[a * 3 + 2 - s, :, :256], NT)
            total += dot(rem[rows].reshape(512, 256), wrem[wr, a], NT)
        return total

    def widened(dst):
        @pl.loop(0, 2)
        def _(h):
            for yy in range(4):
                lo, hi = (128, 320) if yy == 3 else (0, 256)
                total = jnp.zeros((544, 256), F32)
                for s in range(3):
                    cells = sh[s, pl.ds(h * 17, 17)].reshape(544, C)[:, lo:hi]
                    total += dot(cells, pmat[yy * 3 + s, : hi - lo])
                dst[yy, pl.ds(h * 544, 544), :] = total.astype(BF16)

    def turned(src):
        for n in range(4):
            gt[:, n * 256 : (n + 1) * 256] = dot(omat[...], src[n * 256 : (n + 1) * 256, :], NT).astype(BF16)

    def put(dst, yy, base, value):
        value = value.astype(BF16)
        for half in range(2):
            for q in range(2):
                for h in range(2):
                    dst[half, yy, h * 2 + q, pl.ds(base, 80), :] = value[
                        half * 160 + q * 80 : half * 160 + (q + 1) * 80, h * 128 : (h + 1) * 128
                    ]

    def weights(dst, src):
        @pl.loop(0, 3)
        def _(a):
            for yy in range(4):
                put(dst, yy, a * 80, dot(gt[...], src[yy, pl.ds(a * T, 1024), :]))

    landed(first)
    shifted(0, False, True)
    loads[4].wait()
    loads[5].wait()

    @pl.loop(0, 2)
    def _(h):
        grad = conv(wd, 0, h * 16)
        grad = (slope(pre[pl.ds(h * 16, 16)].reshape(512, C).astype(F32)) * grad).astype(BF16)
        dec[pl.ds(h * 512, 512), :] = grad
        in4[3, pl.ds(h * 16, 16)] = dot(grad, wz[...], NT).astype(BF16).reshape(16, T, C)

    scol[0, 3] = in4[3, :, 0, :]
    scol[1, 3] = in4[3, :, T - 1, :]
    second = halo(3, 1, 1)
    start(second)

    shifted(1, True, False)
    widened(xmid)
    turned(in4[3].reshape(1024, C))
    weights(ra, xmid)

    loads[6].wait()
    turned(dec)
    for yy in range(4):
        lo, hi = (128, 320) if yy == 3 else (0, 256)
        xout[...] = dot(cout[...].reshape(1024, C)[:, lo:hi], pmat[yy * 3, : hi - lo]).astype(BF16)
        put(ra, yy, 240, dot(gt[...], xout[...]))

    def pair(src, dst, n):
        return pltpu.make_async_remote_copy(
            src_ref=src, dst_ref=dst, send_sem=cs_sem.at[n], recv_sem=cr_sem.at[n],
            device_id=partner, device_id_type=MESH,
        )

    def remote(src, dst, n, peer):
        return pltpu.make_async_remote_copy(
            src_ref=src, dst_ref=dst, send_sem=ss_sem.at[n], recv_sem=sr_sem.at[n],
            device_id=peer, device_id_type=MESH,
        )

    class Stage:
        def __init__(self, base, pn, rows, split, zn, bufs, out, zt):
            self.base, self.pn, self.rows, self.split, self.zn = base, pn, rows, split, zn
            (self.r, self.c, self.y, self.x, self.e, self.f, self.y2, self.x2,
             self.d, self.zs, self.zr, self.fin, self.pin) = bufs
            self.out, self.zt = out, zt
            self.sent = []

        def go(self, copies):
            for copy in copies:
                copy.start()
            self.sent += copies
            return copies

        def one(self):
            self.k1 = self.go([pair(self.r.at[1 - core], self.c, self.pn)])

        def two(self):
            self.k1[0].wait_recv()

            @pl.loop(0, 4)
            def _(t):
                for u in range(4):
                    self.r[core, t, u] = (
                        self.r[core, t, u].astype(F32) + self.c[t, u].astype(F32)
                    ).astype(BF16)

            lo, hi = pl.ds(0, self.split), pl.ds(self.split, self.rows - self.split)
            self.k2 = []
            for d in (2, 1, 3):
                ty, tx = (y + d) % 4, (x + d) % 4
                self.k2.append(remote(self.r.at[core, ty, :, lo], self.y.at[d - 1], self.base + d - 1, at_y(ty)))
                self.k2.append(remote(self.r.at[core, :, tx, hi], self.x.at[d - 1], self.base + 2 + d, at_x(tx)))
            self.go(self.k2)

        def three(self):
            for copy in self.k2:
                copy.wait_recv()
            lo, hi = pl.ds(0, self.split), pl.ds(self.split, self.rows - self.split)

            @pl.loop(0, 4)
            def _(t):
                total = self.r[core, y, t, lo].astype(F32)
                for d in range(3):
                    total += self.y[d, t].astype(F32)
                self.e[t] = total.astype(BF16)
                total = self.r[core, t, x, hi].astype(F32)
                for d in range(3):
                    total += self.x[d, t].astype(F32)
                self.f[t] = total.astype(BF16)

            self.k3 = []
            for d in (2, 1, 3):
                ty, tx = (y + d) % 4, (x + d) % 4
                self.k3.append(remote(self.e.at[tx], self.x2.at[d - 1], self.base + 5 + d, at_x(tx)))
                self.k3.append(remote(self.f.at[ty], self.y2.at[d - 1], self.base + 8 + d, at_y(ty)))
            self.go(self.k3)

        def four(self):
            for copy in self.k3:
                copy.wait_recv()
            total = self.e[x].astype(F32)
            for d in range(3):
                total += self.x2[d].astype(F32)
            self.d[0 : self.split] = total.astype(BF16)
            total = self.f[y].astype(F32)
            for d in range(3):
                total += self.y2[d].astype(F32)
            self.d[self.split : self.rows] = total.astype(BF16)
            pick = jnp.where(
                lax.broadcasted_iota(jnp.int32, (8 * self.zn, self.rows), 1) == self.zt[...], 1.0, 0.0
            ).astype(BF16)
            self.zs[...] = dot(pick, self.d[...]).astype(BF16).reshape(8, self.zn, 128)
            self.k4 = []
            for d in (4, 3, 5, 2, 6, 1, 7):
                tz = (z + d) % 8
                self.k4.append(remote(self.zs.at[tz], self.zr.at[d - 1], self.base + 11 + d, at_z(tz)))
            self.go(self.k4)

        def five(self):
            for copy in self.k4:
                copy.wait_recv()
            total = self.zs[z].astype(F32)
            for d in range(7):
                total += self.zr[d].astype(F32)
            self.fin[...] = total
            self.out[core] = total
            self.k5 = self.go([pair(self.fin, self.pin, self.pn + 1)])

        def six(self):
            self.k5[0].wait_recv()
            self.out[1 - core] = self.pin[...]

    stage_a = Stage(0, 0, ROWS_A, SPLIT_A, ZA, (ra, ca, ya, xa, ea, fa, ya2, xa2, da, zsa, zra, fina, pina), out_a, za_ref)
    stage_b = Stage(19, 2, ROWS_B, SPLIT_B, ZB, (rb, cb, yb, xb, eb, fb, yb2, xb2, db, zsb, zrb, finb, pinb), out_b, zb_ref)

    stage_a.one()

    shifted(2, True, False)
    widened(xin)

    stage_a.two()

    loads[7].wait()
    for a in range(3):
        for b in range(3):
            wrem[1, a, :, (2 - b) * 64 : (3 - b) * 64] = wc[a * 3 + b, :, 256:320]
        wrem[1, a, :, 192:256] = jnp.zeros((C, 64), BF16)

    landed(second)
    shifted(3, False, True)

    @pl.loop(0, 2)
    def _(h):
        grad = conv(wc, 1, h * 16)
        grad = slope(in4[1, pl.ds(h * 16, 16)].reshape(512, C).astype(F32)) * grad
        mgrad[pl.ds(h * 512, 512), :] = grad.astype(BF16)

    turned(mgrad)
    weights(rb, xin)

    stage_b.one()
    stage_a.three()
    stage_b.two()
    stage_a.four()
    stage_b.three()
    stage_a.five()
    stage_b.four()
    stage_a.six()
    stage_b.five()
    stage_b.six()

    for copies in (first, second):
        for d, copy in copies:
            pl.when(there[d])(copy.wait_send)
    for copy in stage_a.sent + stage_b.sent:
        copy.wait_send()


def stage_buffers(rows, split, zn):
    rest = rows - split
    return [
        pltpu.VMEM((2, 4, 4, rows, 128), BF16),
        pltpu.VMEM((4, 4, rows, 128), BF16),
        pltpu.VMEM((3, 4, split, 128), BF16),
        pltpu.VMEM((3, 4, rest, 128), BF16),
        pltpu.VMEM((4, split, 128), BF16),
        pltpu.VMEM((4, rest, 128), BF16),
        pltpu.VMEM((3, rest, 128), BF16),
        pltpu.VMEM((3, split, 128), BF16),
        pltpu.VMEM((rows, 128), BF16),
        pltpu.VMEM((8, zn, 128), BF16),
        pltpu.VMEM((7, zn, 128), BF16),
        pltpu.VMEM((zn, 128), F32),
        pltpu.VMEM((zn, 128), F32),
    ]


def on_device(grad_out, dec_pre, ctrl_out, ctrl_mid, ctrl_in, dec_weight, zero_weight, ctrl_weight):
    tabs = [jnp.asarray(t) for t in tables()]
    anys = pl.BlockSpec(memory_space=pl.ANY)
    vmem = pl.BlockSpec(memory_space=pltpu.VMEM)
    out_a, out_b = pl.pallas_call(
        kernel,
        out_shape=(
            jax.ShapeDtypeStruct((2, ZA, 128), F32),
            jax.ShapeDtypeStruct((2, ZB, 128), F32),
        ),
        in_specs=[anys] * 8 + [vmem] * 4,
        out_specs=(vmem, vmem),
        scratch_shapes=[
            pltpu.VMEM((4, T, T, C), BF16),
            pltpu.VMEM((T, T, C), BF16),
            pltpu.VMEM((T, T, C), BF16),
            pltpu.VMEM((9, C, C), BF16),
            pltpu.VMEM((C, C), BF16),
            pltpu.VMEM((9, C, C), BF16),
            pltpu.VMEM((2, 4, T, C), BF16),
            pltpu.VMEM((2, 4, T, C), BF16),
            pltpu.VMEM((2, 4, T, C), BF16),
            pltpu.VMEM((4, 4, 16, C), BF16),
            pltpu.VMEM((2, 40, C), F32),
            pltpu.VMEM((3, T + 2, T, C), BF16),
            pltpu.VMEM((T + 2, T, 256), BF16),
            pltpu.VMEM((2, 3, C, 256), BF16),
            pltpu.VMEM((1024, C), BF16),
            pltpu.VMEM((4, 1088, 256), BF16),
            pltpu.VMEM((4, 1088, 256), BF16),
            pltpu.VMEM((1024, 256), BF16),
            pltpu.VMEM((12, 256, 256), BF16),
            pltpu.VMEM((C, C), BF16),
            pltpu.VMEM((C, 1024), BF16),
            pltpu.VMEM((1024, C), BF16),
        ]
        + stage_buffers(ROWS_A, SPLIT_A, ZA)
        + stage_buffers(ROWS_B, SPLIT_B, ZB)
        + [
            pltpu.SemaphoreType.DMA((8,)),
            pltpu.SemaphoreType.DMA((2, 8)),
            pltpu.SemaphoreType.DMA((2, 8)),
            pltpu.SemaphoreType.DMA((4,)),
            pltpu.SemaphoreType.DMA((4,)),
            pltpu.SemaphoreType.DMA((38,)),
            pltpu.SemaphoreType.DMA((38,)),
        ],
        compiler_params=pltpu.CompilerParams(
            collective_id=0, has_side_effects=True, vmem_limit_bytes=60 * 1024 * 1024
        ),
        name="fused",
    )(
        grad_out, dec_pre, ctrl_out, ctrl_mid, ctrl_in,
        dec_weight.reshape(9, C, C), zero_weight, ctrl_weight.reshape(9, C, C), *tabs,
    )
    core = lax.axis_index("row") % 2
    out_a = lax.dynamic_slice_in_dim(out_a, core * 64, 64, axis=2)
    out_b = lax.dynamic_slice_in_dim(out_b, core * 64, 64, axis=2)
    both = jnp.concatenate([out_a[:, :30, :60], out_b[:, :30, :60]], axis=1)
    both = both.reshape(2, 2, 3, 10, 3, 20).transpose(1, 2, 4, 5, 0, 3).reshape(2, 3, 3, 20, 20)
    grad_zero = out_a[:, 30:40, :20].transpose(2, 0, 1).reshape(20, 20)
    return (grad_zero, both[0], both[1])


def solution(mesh):
    tile = P("row", "col", None)
    return jax.shard_map(
        on_device,
        mesh=mesh,
        in_specs=(tile,) * 5 + (P(),) * 3,
        out_specs=(P("row", "col"), P(None, None, "row", "col"), P(None, None, "row", "col")),
        check_vma=False,
    )
```

time: 282 us -> 74.6 us (0.26)
  waiting for transfers between devices: 122 us -> 0 us
  Pallas kernels: 0 us -> 69.4 us
  matrix products: 36.8 us -> 0 us
  starting transfers between devices: 34.3 us -> 0 us
  local copies, waits for them, and re-layouts: 32.5 us -> 4.25 us
  other arithmetic: 19.9 us -> 0.01 us
  blocking collectives: 18.9 us -> 0 us
  between operations: 14.6 us -> 0.7 us
    reduce_scatter x1 -> x0, waiting for transfers between devices: 105 us -> none  [on_device(): lax.psum_scatter(stacked.astype(jnp.bfloat16), 'row', scatter_dimension=1...]
    pallas_call x0 -> x1, Pallas kernels: none -> 69.4 us  [on_device(): pl.pallas_call(kernel, out_shape=(jax.ShapeDtypeStruct((2, ZA, 128), F32)...]
    dot_general x38 -> x0, matrix products: 36.8 us -> none  [the longest x18 24.2 us: weight_local(): lax.dot_general(window, flat_grad, (((0,), (0,)), ((), ())), preferred_el...]
    ppermute x12 -> x0, starting transfers between devices: 34.3 us -> none  [the longest x6 24.5 us: with_halo(): lax.ppermute(tail, axis, [(i, (i + 1) % count) for i in range(ends)])]
    all_to_all x1 -> x0, blocking collectives: 18.9 us -> none  [sent_and_summed(): lax.all_to_all(blocks, axis, split_axis=0, concat_axis=0, tiled=True)]
    ppermute x12 -> x0, waiting for transfers between devices: 17 us -> none  [the longest x6 16.4 us: with_halo(): lax.ppermute(head, axis, [((i + 1) % count, i) for i in range(ends)])]
    concatenate x8 -> x1, other arithmetic: 9.99 us -> 0.01 us  [on_device(): both = jnp.concatenate([out_a[:, :30, :60], out_b[:, :30, :60]], axis=1)]
    concatenate x2 -> x1, local copies, waits for them, and re-layouts: 8.91 us -> 0.05 us  [on_device(): both = jnp.concatenate([out_a[:, :30, :60], out_b[:, :30, :60]], axis=1)]
  transfers between devices with their start and end apart: 13 -> 0, of which waited for: 7 -> 0; matrix products, arithmetic and copies ran while one was open for 2% -> 0% of each run, Pallas kernels for 0% -> 0%
where the time goes in v1:
time: 74.6 us; the launch traced here: 74.4 us
  Pallas kernels  69.4 us (93%)
  local copies, waits for them, and re-layouts  4.25 us (6%)
    pallas_call x1, Pallas kernels, on_device(): pl.pallas_call(kernel, out_shape=(jax.ShapeDtypeStruct((2, ZA, 128), F32)...  69.4 us
    unnamed x3, local copies, waits for them, and re-layouts  2.26 us

profile of v1, /device:TPU:1, one launch (start us, length us, event | category | flops | bytes accessed | tf_op | source)
XLA Modules:
  0.0 74.4 jit_solution(4981069443484855119)
XLA Ops:
  0.6 69.4 %fused.1 = (f32[2,48,128]{2,1,0:T(8,128)}, f32[2,32,128]{2,1,0:T(8,128)}) custom-call(bf16[32,32,320]{2,1,0:T(8,128)(2,1)} %g_hbm.1, bf16[32,32,320]{2,1,0:T(8,128)(2,1)} %pre_hbm.1, bf16[32,32,320]{2,1,0:T(8,128)(2,1)} %cout_hbm.1, bf16[32,32,320]{2,1,0:T(8,128)(2,1)} %mid_hbm.1, bf16[32,32,320]{2,1,0:T(8,128)(2,1)} %cin_hbm.1, ...), custom_call_target="tpu_custom_call" | custom-call | tf_op jit(solution)/shard_map/fused/pallas_call | solution.py:487
  70.1 0.8 %dynamic-slice_bitcast_fusion = f32[20,2,10]{0,2,1:T(8,128)S(1)} fusion(f32[2,48,128]{2,1,0:T(8,128)} %get-tuple-element.5, s32[]{:T(128)S(6)} %add.10, s32[]{:T(128)S(6)} %select_n.12), kind=kLoop, calls=%fused_computation.1 | loop fusion | bytes 3208 | tf_op jit(solution)/shard_map/transpose | solution.py:543
  70.9 0.9 %constant_dynamic-slice_fusion = (f32[2,30,60]{2,1,0:T(8,128)S(1)}, f32[2,30,60]{2,1,0:T(8,128)S(1)}) fusion(f32[2,32,128]{2,1,0:T(8,128)} %get-tuple-element.6, s32[]{:T(128)S(6)} %select_n.12, f32[2,48,128]{2,1,0:T(8,128)} %get-tuple-element.5), kind=kLoop, calls=%fused_computation.2 | loop fusion | bytes 57604 | tf_op jit(solution)/shard_map/slice | solution.py:541
  71.7 0.7 copy.21
  72.5 0.1 copy.18
  72.5 0.2 reshape.26
  72.8 0.8 %copy.23 = f32[3,3,20,20]{3,2,1,0:T(8,128)} copy(f32[3,3,20,20]{2,1,3,0:T(4,128)S(1)} %bitcast.14) | data formatting | bytes 28800
  73.6 0.8 %copy.22 = f32[3,3,20,20]{3,2,1,0:T(8,128)} copy(f32[3,3,20,20]{2,1,3,0:T(4,128)S(1)} %bitcast.15) | data formatting | bytes 28800
  (5 shorter events, 0.1 us)

commit v2 on v1

v2 whole, which is shorter than its diff:
```python
import jax
import jax.numpy as jnp
import numpy as np
from jax import lax
from jax.experimental import pallas as pl
from jax.experimental.pallas import tpu as pltpu
from jax.sharding import PartitionSpec as P

F32 = jnp.float32
BF16 = jnp.bfloat16
MESH = pl.DeviceIdType.MESH
NT = (((1,), (1,)), ((), ()))
NN = (((1,), (0,)), ((), ()))
C = 320
T = 32
ZA, ZB1, ZB2 = 48, 32, 16
N_SEM = 80


def dot(a, b, dims=NN):
    return lax.dot_general(a, b, dims, preferred_element_type=F32)


def silu(v):
    return v * jax.nn.sigmoid(v)


def slope(v):
    s = jax.nn.sigmoid(v)
    return s * (1.0 + v * (1.0 - s))


def tables():
    place = np.full((16, 256), -1, np.int32)
    for y in range(4):
        for s in range(3):
            for xh in range(2):
                for core in range(2):
                    for i in range(20):
                        lane = xh * 128 + core * 64 + s * 20 + i
                        c = y * 80 + xh * 40 + core * 20 + i
                        if c < 256:
                            place[y * 3 + s, lane] = c
                        else:
                            place[12, lane] = s * 64 + c - 256
    order = np.zeros((C, 1), np.int32)
    for core in range(2):
        for xl in range(2):
            for z in range(8):
                for i in range(10):
                    order[core * 160 + xl * 80 + z * 10 + i, 0] = (xl * 8 + z) * 20 + core * 10 + i
    deals = []
    for zn, groups in ((ZA, 4), (ZB1, 2), (ZB2, 1)):
        deal = np.full((8 * zn, 1), -1, np.int32)
        for z in range(8):
            for g in range(groups):
                for i in range(10):
                    deal[z * zn + g * 10 + i, 0] = g * 80 + z * 10 + i
        deals.append(deal)
    return place, order, *deals


def kernel(
    g_hbm, pre_hbm, cout_hbm, mid_hbm, cin_hbm, wd_hbm, wz_hbm, wc_hbm,
    place_hbm, order_hbm, deal_a_hbm, deal_b1_hbm, deal_b2_hbm,
    out_a, out_b1, out_b2,
    place_ref, order_ref, deal_a, deal_b1, deal_b2,
    in4, pre, cout, wd, wz, wc,
    scol, hrow, hcol, hcor, hc32,
    shg, remg, shm, remm, shi, remi,
    wrem, wn, tails, dec, pmat, omat, gt, mgrad,
    ra, rz, rb1, rb2,
    *rest,
):
    bufs, (load_sem, hs_sem, hr_sem, send_sem, recv_sem) = rest[:-5], rest[-5:]
    row = lax.axis_index("row")
    col = lax.axis_index("col")
    y, xh, core = row // 4, (row // 2) % 2, row % 2
    xl, z = col // 8, col % 8
    x = xh * 2 + xl

    def at_y(t):
        return ((t * 2 + xh) * 2 + core, col)

    def at_x(t):
        return ((y * 2 + t // 2) * 2 + core, (t % 2) * 8 + z)

    def at_z(t):
        return (row, xl * 8 + t)

    partner = (row + 1 - 2 * core, col)

    loads = [
        pltpu.make_async_copy(g_hbm, in4.at[0], load_sem.at[0]),
        pltpu.make_async_copy(mid_hbm, in4.at[1], load_sem.at[1]),
        pltpu.make_async_copy(cin_hbm, in4.at[2], load_sem.at[2]),
        pltpu.make_async_copy(wd_hbm, wd, load_sem.at[3]),
        pltpu.make_async_copy(pre_hbm, pre, load_sem.at[4]),
        pltpu.make_async_copy(wz_hbm, wz, load_sem.at[5]),
        pltpu.make_async_copy(wc_hbm, wc, load_sem.at[6]),
        pltpu.make_async_copy(cout_hbm, cout, load_sem.at[7]),
        pltpu.make_async_copy(order_hbm, order_ref, load_sem.at[8]),
        pltpu.make_async_copy(place_hbm, place_ref, load_sem.at[9]),
        pltpu.make_async_copy(deal_a_hbm, deal_a, load_sem.at[10]),
        pltpu.make_async_copy(deal_b1_hbm, deal_b1, load_sem.at[11]),
        pltpu.make_async_copy(deal_b2_hbm, deal_b2, load_sem.at[12]),
    ]
    for copy in loads:
        copy.start()

    has = {-1: (row > 0, col > 0), 1: (row < 15, col < 15), 0: (row >= 0, col >= 0)}
    around = [(dr, dc) for dr in (-1, 0, 1) for dc in (-1, 0, 1) if (dr, dc) != (0, 0)]
    there = {d: jnp.logical_and(has[d[0]][0], has[d[1]][1]) for d in around}

    barrier = pltpu.get_barrier_semaphore()
    for d in around:
        @pl.when(there[d])
        def _(d=d):
            pl.semaphore_signal(barrier, inc=1, device_id=(row + d[0], col + d[1]), device_id_type=MESH)
    peers = [partner]
    peers += [at_y((y + d) % 4) for d in range(1, 4)]
    peers += [at_x((x + d) % 4) for d in range(1, 4)]
    peers += [at_z((z + d) % 8) for d in range(1, 8)]
    for peer in peers:
        pl.semaphore_signal(barrier, inc=1, device_id=peer, device_id_type=MESH)

    def sides(n):
        scol[0, n] = in4[n, :, 0, :]
        scol[1, n] = in4[n, :, T - 1, :]

    loads[0].wait()
    sides(0)

    count = jnp.int32(len(peers))
    for d in around:
        count = count + there[d].astype(jnp.int32)
    pl.semaphore_wait(barrier, count)

    def halo(first, size, phase):
        copies = []
        for n, (dr, dc) in enumerate(around):
            span = pl.ds(first, size)
            if dc == 0:
                src = in4.at[span, 0 if dr < 0 else T - 1]
                dst = hrow.at[1 if dr < 0 else 0, span]
            elif dr == 0:
                src = scol.at[0 if dc < 0 else 1, span]
                dst = hcol.at[1 if dc < 0 else 0, span]
            else:
                src = scol.at[0 if dc < 0 else 1, span, pl.ds(0 if dr < 0 else 16, 16)]
                dst = hcor.at[(1 if dr < 0 else 0) * 2 + (1 if dc < 0 else 0), span]
            copies.append(
                (
                    (dr, dc),
                    pltpu.make_async_remote_copy(
                        src_ref=src, dst_ref=dst,
                        send_sem=hs_sem.at[phase, n], recv_sem=hr_sem.at[phase, n],
                        device_id=(row + dr, col + dc), device_id_type=MESH,
                    ),
                )
            )
        return copies

    def start(copies):
        for d, copy in copies:
            pl.when(there[d])(copy.start)

    def landed(copies):
        for d, copy in copies:
            pl.when(there[(-d[0], -d[1])])(copy.wait_recv)

    first = halo(0, 1, 0)
    start(first)
    loads[1].wait()
    loads[2].wait()
    sides(1)
    sides(2)
    acts = halo(1, 2, 1)
    start(acts)

    def clear(condition, ref, slot):
        @pl.when(condition)
        def _():
            ref[slot] = jnp.zeros(ref.shape[1:], BF16)

    clear(row == 0, hrow, 0)
    clear(row == 15, hrow, 1)
    clear(col == 0, hcol, 0)
    clear(col == 15, hcol, 1)
    for slot in range(4):
        edge_row = row == (0 if slot < 2 else 15)
        edge_col = col == (0 if slot % 2 == 0 else 15)
        clear(jnp.logical_or(edge_row, edge_col), hcor, slot)

    edge = lax.broadcasted_iota(jnp.int32, (T, C), 0)
    half_edge = lax.broadcasted_iota(jnp.int32, (16, C), 0)

    def columns(k, act):
        for side in range(2):
            parts = (hcor[side, k].astype(F32), hcol[side, k].astype(F32), hcor[2 + side, k].astype(F32))
            if act:
                parts = [silu(v) for v in parts]
            hc32[side, 0:1, :] = parts[0][15:16]
            hc32[side, 1:33, :] = parts[1]
            hc32[side, 33:34, :] = parts[2][0:1]

    def emit(sh, i, cells, act, sides):
        now = cells.astype(F32)
        if act:
            now = silu(now)
        minus, plus = pltpu.roll(now, 1, 0), pltpu.roll(now, T - 1, 0)
        if sides:
            minus = jnp.where(edge == 0, hc32[0, pl.ds(i, 1), :], minus)
            plus = jnp.where(edge == T - 1, hc32[1, pl.ds(i, 1), :], plus)
        sh[0, i] = minus.astype(BF16)
        sh[1, i] = now.astype(BF16)
        sh[2, i] = plus.astype(BF16)

    def inner(sh, k, act, sides):
        @pl.loop(0, T, unroll=4)
        def _(i):
            emit(sh, i + 1, in4[k, i], act, sides)

    def outer(sh, k, act):
        emit(sh, 0, hrow[0, k], act, True)
        emit(sh, T + 1, hrow[1, k], act, True)

    def patch(sh):
        @pl.loop(1, T + 1, unroll=4)
        def _(i):
            cells = sh[0, i, 0:16, :].astype(F32)
            sh[0, i, 0:16, :] = jnp.where(half_edge == 0, hc32[0, pl.ds(i, 1), :], cells).astype(BF16)
            cells = sh[2, i, 16:32, :].astype(F32)
            sh[2, i, 16:32, :] = jnp.where(half_edge == 15, hc32[1, pl.ds(i, 1), :], cells).astype(BF16)

    def gather_rem(sh, rem):
        @pl.loop(0, 2 * (T + 2) // 4)
        def _(n):
            span = pl.ds(n * 2, 2)
            for s in range(3):
                rem[span, :, s * 64 : (s + 1) * 64] = sh[s, span, :, 256:320]
            rem[span, :, 192:256] = jnp.zeros((2, T, 64), BF16)

    def arrange(w, slot):
        for a in range(3):
            for b in range(3):
                wrem[slot, a, :, (2 - b) * 64 : (3 - b) * 64] = w[a * 3 + b, :, 256:320]
                wn[slot, 2 - b, a * 64 : (a + 1) * 64, :] = w[a * 3 + b, 256:320, :256]
            wrem[slot, a, :, 192:256] = jnp.zeros((C, 64), BF16)
            wn[slot, 3, a * 64 : (a + 1) * 64, :] = wrem[slot, a, 256:320, :]
        wn[slot, :, 192:256, :] = jnp.zeros((4, 64, 256), BF16)

    def conv_tails(slot):
        @pl.loop(0, 2)
        def _(h):
            span = pl.ds(h * 17, 17)
            total = dot(remg[span].reshape(544, 256), wn[slot, 3], NT)
            for s in range(3):
                total += dot(shg[s, span].reshape(544, C)[:, :256], wn[slot, s], NT)
            tails[span] = total.reshape(17, T, 256)

    def conv(w, slot, i0):
        total = jnp.zeros((512, 256), F32)
        for a in range(3):
            span = pl.ds(i0 + 2 - a, 16)
            for s in range(3):
                total += dot(shg[s, span].reshape(512, C)[:, :256], w[a * 3 + 2 - s, :256, :256], NT)
            total += dot(remg[span].reshape(512, 256), wrem[slot, a, :256, :], NT)
        last = (
            tails[pl.ds(i0 + 2, 16)].reshape(512, 256)[:, :64]
            + tails[pl.ds(i0 + 1, 16)].reshape(512, 256)[:, 64:128]
            + tails[pl.ds(i0, 16)].reshape(512, 256)[:, 128:192]
        )
        return total, last

    def turned(src):
        for n in range(4):
            gt[:, n * 256 : (n + 1) * 256] = dot(omat[...], src[n * 256 : (n + 1) * 256, :], NT).astype(BF16)

    def halves(dst, base, lane, width, value):
        value = value.astype(BF16)
        for half in range(2):
            dst[half, base : base + 160, lane : lane + width] = value[half * 160 : (half + 1) * 160]

    def weights(dst, base, sh, rem, a):
        span = pl.ds(a, T)
        for s in range(3):
            halves(dst, base, s * 256, 256, dot(gt[...], sh[s, span].reshape(1024, C)[:, :256]))
        halves(dst, base, 768, 256, dot(gt[...], rem[span].reshape(1024, 256)))

    counter = [0]

    def remote(src, dst, peer):
        n = counter[0]
        counter[0] += 1
        return pltpu.make_async_remote_copy(
            src_ref=src, dst_ref=dst, send_sem=send_sem.at[n], recv_sem=recv_sem.at[n],
            device_id=peer, device_id_type=MESH,
        )

    class Stage:
        def __init__(self, out, deal, zn, sources, groups, rows, split, mine):
            self.out, self.deal, self.zn, self.sources, self.groups = out, deal, zn, sources, groups
            self.rows, self.split = rows, split
            self.landings = mine[: len(sources)]
            (self.d, self.ha, self.hb, self.pa, self.pb, self.e, self.f, self.ea, self.fb,
             self.j, self.zs, self.zr, self.fin, self.pin) = mine[len(sources):]
            self.sent = []

        def go(self, *copies):
            for copy in copies:
                copy.start()
            self.sent += copies
            return copies

        def one(self):
            self.k1 = self.go(*[
                remote(src.at[1 - core], dst, partner) for src, dst in zip(self.sources, self.landings)
            ])

        def put(self, base, yy, value):
            value = value.astype(BF16)
            for q in range(2):
                for h in range(2):
                    self.d[yy, h * 2 + q, pl.ds(base, 80), :] = value[
                        q * 80 : (q + 1) * 80, h * 128 : (h + 1) * 128
                    ]

        def two(self):
            for copy in self.k1:
                copy.wait_recv()

            def both(n, span, lanes):
                here = self.sources[n][core, span, lanes].astype(F32)
                return (here + self.landings[n][span, lanes].astype(F32)).astype(BF16)

            for g in range(self.groups):
                span = slice(g * 160, (g + 1) * 160)
                parts = [both(0, span, slice(s * 256, (s + 1) * 256)) for s in range(4)]
                for yy in range(4):
                    total = dot(parts[0], pmat[yy * 3])
                    for s in range(1, 3):
                        total += dot(parts[s], pmat[yy * 3 + s])
                    if yy == 3:
                        total += dot(parts[3], pmat[12])
                    self.put(g * 80, yy, total)
            if len(self.sources) > 1:
                main, last = (both(1, slice(0, 160), lanes) for lanes in (slice(0, 256), slice(256, 320)))
                for yy in range(4):
                    total = dot(main, pmat[yy * 3])
                    if yy == 3:
                        total += dot(last, pmat[12, 0:64])
                    self.put(self.groups * 80, yy, total)

            lo, hi = pl.ds(0, self.split), pl.ds(self.split, self.rows - self.split)
            far_y, far_x = (y + 2) % 4, (x + 2) % 4
            up_y, down_y, up_x, down_x = (y + 1) % 4, (y + 3) % 4, (x + 1) % 4, (x + 3) % 4
            low, high = pl.ds(0, 2), pl.ds(2, 2)
            self.k2 = self.go(
                remote(self.d.at[far_y, low, lo], self.ha.at[0], at_y(up_y)),
                remote(self.d.at[far_y, high, lo], self.ha.at[1], at_y(down_y)),
                remote(self.d.at[low, far_x, hi], self.hb.at[0], at_x(up_x)),
                remote(self.d.at[high, far_x, hi], self.hb.at[1], at_x(down_x)),
            )

        def relay(self):
            for copy in self.k2:
                copy.wait_recv()
            lo, hi = pl.ds(0, self.split), pl.ds(self.split, self.rows - self.split)
            for n in range(2):
                ty, tx = (y + 1 + 2 * n) % 4, (x + 1 + 2 * n) % 4
                for u in range(2):
                    t = 2 * n + u
                    self.d[ty, t, lo] = (self.d[ty, t, lo].astype(F32) + self.ha[n, u].astype(F32)).astype(BF16)
                    self.d[t, tx, hi] = (self.d[t, tx, hi].astype(F32) + self.hb[n, u].astype(F32)).astype(BF16)
            self.k3 = []
            for n in range(2):
                ty, tx = (y + 1 + 2 * n) % 4, (x + 1 + 2 * n) % 4
                self.k3 += self.go(
                    remote(self.d.at[ty, :, lo], self.pa.at[n], at_y(ty)),
                    remote(self.d.at[:, tx, hi], self.pb.at[n], at_x(tx)),
                )

        def three(self):
            for copy in self.k3:
                copy.wait_recv()
            lo, hi = pl.ds(0, self.split), pl.ds(self.split, self.rows - self.split)
            for t in range(4):
                total = self.d[y, t, lo].astype(F32) + self.pa[0, t].astype(F32) + self.pa[1, t].astype(F32)
                self.e[t] = total.astype(BF16)
                total = self.d[t, x, hi].astype(F32) + self.pb[0, t].astype(F32) + self.pb[1, t].astype(F32)
                self.f[t] = total.astype(BF16)
            self.k4 = []
            for d in (2, 1, 3):
                ty, tx = (y + d) % 4, (x + d) % 4
                self.k4 += self.go(
                    remote(self.e.at[tx], self.ea.at[d - 1], at_x(tx)),
                    remote(self.f.at[ty], self.fb.at[d - 1], at_y(ty)),
                )

        def four(self):
            for copy in self.k4:
                copy.wait_recv()
            total = self.e[x].astype(F32)
            for d in range(3):
                total += self.ea[d].astype(F32)
            self.j[0 : self.split] = total.astype(BF16)
            total = self.f[y].astype(F32)
            for d in range(3):
                total += self.fb[d].astype(F32)
            self.j[self.split : self.rows] = total.astype(BF16)
            pick = jnp.where(
                lax.broadcasted_iota(jnp.int32, (8 * self.zn, self.rows), 1) == self.deal[...], 1.0, 0.0
            ).astype(BF16)
            self.zs[...] = dot(pick, self.j[...]).astype(BF16).reshape(8, self.zn, 128)
            self.k5 = []
            for d in (4, 3, 5, 2, 6, 1, 7):
                tz = (z + d) % 8
                self.k5 += self.go(remote(self.zs.at[tz], self.zr.at[d - 1], at_z(tz)))

        def five(self):
            for copy in self.k5:
                copy.wait_recv()
            total = self.zs[z].astype(F32)
            for d in range(7):
                total += self.zr[d].astype(F32)
            self.fin[...] = total
            self.k6 = self.go(remote(self.fin, self.pin, partner))
            self.show(core, total)

        def show(self, side, value):
            self.out[side] = jnp.where(core == 0, value[:, :64], value[:, 64:])

        def six(self):
            self.k6[0].wait_recv()
            self.show(1 - core, self.pin[...])

    stage_a = Stage(out_a, deal_a, ZA, (ra, rz), 3, 320, 160, bufs[0:16])
    stage_b1 = Stage(out_b1, deal_b1, ZB1, (rb1,), 2, 160, 80, bufs[16:31])
    stage_b2 = Stage(out_b2, deal_b2, ZB2, (rb2,), 1, 80, 48, bufs[31:46])

    loads[3].wait()
    arrange(wd, 0)
    inner(shg, 0, False, False)
    landed(first)
    columns(0, False)
    outer(shg, 0, False)
    patch(shg)
    gather_rem(shg, remg)
    loads[4].wait()
    loads[5].wait()
    conv_tails(0)

    @pl.loop(0, 2)
    def _(h):
        main, last = conv(wd, 0, h * 16)
        rate = slope(pre[pl.ds(h * 16, 16)].reshape(512, C).astype(F32))
        dec[pl.ds(h * 512, 512), 0:256] = (rate[:, :256] * main).astype(BF16)
        dec[pl.ds(h * 512, 512), 256:320] = (rate[:, 256:] * last).astype(BF16)
        grad = dec[pl.ds(h * 512, 512), :]
        in4[3, pl.ds(h * 16, 16)] = dot(grad, wz[...], NT).astype(BF16).reshape(16, T, C)

    sides(3)
    second = halo(3, 1, 2)
    start(second)

    loads[8].wait()
    omat[...] = jnp.where(
        lax.broadcasted_iota(jnp.int32, (C, C), 1) == order_ref[...], 1.0, 0.0
    ).astype(BF16)
    landed(acts)
    columns(1, True)
    inner(shm, 1, True, True)
    outer(shm, 1, True)
    gather_rem(shm, remm)
    turned(in4[3].reshape(1024, C))
    for a in range(3):
        weights(ra, a * 160, shm, remm, a)
    loads[7].wait()
    turned(dec)
    halves(rz, 0, 0, C, dot(gt[...], cout[...].reshape(1024, C)))
    stage_a.one()
    for n in range(9, 13):
        loads[n].wait()
    depth = lax.broadcasted_iota(jnp.int32, (256, 256), 0)

    @pl.loop(0, 13)
    def _(k):
        pmat[k] = jnp.where(depth == place_ref[pl.ds(k, 1), :], 1.0, 0.0).astype(BF16)

    loads[6].wait()
    arrange(wc, 1)
    inner(shg, 3, False, False)
    landed(second)
    columns(3, False)
    outer(shg, 3, False)
    patch(shg)
    gather_rem(shg, remg)
    stage_a.two()
    columns(2, True)
    inner(shi, 2, True, True)
    outer(shi, 2, True)
    gather_rem(shi, remi)
    conv_tails(1)

    def second_half(h):
        main, last = conv(wc, 1, h * 16)
        rate = slope(in4[1, h * 16 : (h + 1) * 16].reshape(512, C).astype(F32))
        mgrad[h * 512 : (h + 1) * 512, 0:256] = (rate[:, :256] * main).astype(BF16)
        mgrad[h * 512 : (h + 1) * 512, 256:320] = (rate[:, 256:] * last).astype(BF16)

    second_half(0)
    stage_a.relay()
    second_half(1)
    turned(mgrad)
    for a in range(2):
        weights(rb1, a * 160, shi, remi, a)
    stage_b1.one()
    weights(rb2, 0, shi, remi, 2)
    stage_b2.one()
    stage_a.three()
    stage_b1.two()
    stage_b2.two()
    stage_a.four()
    stage_b1.relay()
    stage_b2.relay()
    stage_a.five()
    stage_b1.three()
    stage_b2.three()
    stage_a.six()
    stage_b1.four()
    stage_b2.four()
    stage_b1.five()
    stage_b2.five()
    stage_b1.six()
    stage_b2.six()

    for copies in (first, acts, second):
        for d, copy in copies:
            pl.when(there[d])(copy.wait_send)
    for copy in stage_a.sent + stage_b1.sent + stage_b2.sent:
        copy.wait_send()


def finish(a_ref, b1_ref, b2_ref, zero_ref, ctrl_ref, in_ref):
    def exact(a, b, dims):
        return lax.dot_general(a, b, dims, precision=lax.Precision.HIGHEST, preferred_element_type=F32)

    r = lax.broadcasted_iota(jnp.int32, (72, 64), 0)
    lane = lax.broadcasted_iota(jnp.int32, (72, 64), 1)
    sel = jnp.zeros((72, 64), F32)
    for s in range(3):
        inside = (r >= s * 24) & (r < s * 24 + 20)
        sel = jnp.where(inside & (lane - s * 20 == r - s * 24), 1.0, sel)
    for ref, groups, dst, base in ((a_ref, 4, ctrl_ref, 0), (b1_ref, 2, in_ref, 0), (b2_ref, 1, in_ref, 2)):
        zn = ref.shape[1]
        turn = exact(sel, ref[...].reshape(2 * zn, 64), NT)
        k = lax.broadcasted_iota(jnp.int32, (2 * zn, 20), 0)
        n = lax.broadcasted_iota(jnp.int32, (2 * zn, 20), 1)
        for g in range(groups):
            pick = jnp.where(k == jnp.where(n < 10, n, n - 10 + zn) + g * 10, 1.0, 0.0)
            value = exact(turn, pick, NN)
            if g == 3:
                zero_ref[...] = value[0:20]
            else:
                for s in range(3):
                    dst[(base + g) * 3 + s] = value[s * 24 : s * 24 + 20]


def stage_buffers(landings, rows, split, zn):
    rest = rows - split
    return [pltpu.VMEM(shape, BF16) for shape in landings] + [
        pltpu.VMEM((4, 4, rows, 128), BF16),
        pltpu.VMEM((2, 2, split, 128), BF16),
        pltpu.VMEM((2, 2, rest, 128), BF16),
        pltpu.VMEM((2, 4, split, 128), BF16),
        pltpu.VMEM((2, 4, rest, 128), BF16),
        pltpu.VMEM((4, split, 128), BF16),
        pltpu.VMEM((4, rest, 128), BF16),
        pltpu.VMEM((3, split, 128), BF16),
        pltpu.VMEM((3, rest, 128), BF16),
        pltpu.VMEM((rows, 128), BF16),
        pltpu.VMEM((8, zn, 128), BF16),
        pltpu.VMEM((7, zn, 128), BF16),
        pltpu.VMEM((zn, 128), F32),
        pltpu.VMEM((zn, 128), F32),
    ]


def on_device(grad_out, dec_pre, ctrl_out, ctrl_mid, ctrl_in, dec_weight, zero_weight, ctrl_weight):
    tabs = [jnp.asarray(t) for t in tables()]
    anys = pl.BlockSpec(memory_space=pl.ANY)
    vmem = pl.BlockSpec(memory_space=pltpu.VMEM)
    shifts = [pltpu.VMEM((3, T + 2, T, C), BF16), pltpu.VMEM((T + 2, T, 256), BF16)]
    blocks = pl.pallas_call(
        kernel,
        out_shape=[jax.ShapeDtypeStruct((2, zn, 64), F32) for zn in (ZA, ZB1, ZB2)],
        in_specs=[anys] * 13,
        out_specs=[vmem] * 3,
        scratch_shapes=[
            *[pltpu.VMEM(t.shape, jnp.int32) for t in tabs],
            pltpu.VMEM((4, T, T, C), BF16),
            pltpu.VMEM((T, T, C), BF16),
            pltpu.VMEM((T, T, C), BF16),
            pltpu.VMEM((9, C, C), BF16),
            pltpu.VMEM((C, C), BF16),
            pltpu.VMEM((9, C, C), BF16),
            pltpu.VMEM((2, 4, T, C), BF16),
            pltpu.VMEM((2, 4, T, C), BF16),
            pltpu.VMEM((2, 4, T, C), BF16),
            pltpu.VMEM((4, 4, 16, C), BF16),
            pltpu.VMEM((2, 40, C), F32),
            *shifts, *shifts, *shifts,
            pltpu.VMEM((2, 3, C, 256), BF16),
            pltpu.VMEM((2, 4, 256, 256), BF16),
            pltpu.VMEM((T + 2, T, 256), F32),
            pltpu.VMEM((1024, C), BF16),
            pltpu.VMEM((13, 256, 256), BF16),
            pltpu.VMEM((C, C), BF16),
            pltpu.VMEM((C, 1024), BF16),
            pltpu.VMEM((1024, C), BF16),
            pltpu.VMEM((2, 480, 1024), BF16),
            pltpu.VMEM((2, 160, C), BF16),
            pltpu.VMEM((2, 320, 1024), BF16),
            pltpu.VMEM((2, 160, 1024), BF16),
        ]
        + stage_buffers([(480, 1024), (160, C)], 320, 160, ZA)
        + stage_buffers([(320, 1024)], 160, 80, ZB1)
        + stage_buffers([(160, 1024)], 80, 48, ZB2)
        + [
            pltpu.SemaphoreType.DMA((13,)),
            pltpu.SemaphoreType.DMA((3, 8)),
            pltpu.SemaphoreType.DMA((3, 8)),
            pltpu.SemaphoreType.DMA((N_SEM,)),
            pltpu.SemaphoreType.DMA((N_SEM,)),
        ],
        compiler_params=pltpu.CompilerParams(
            collective_id=0, has_side_effects=True, vmem_limit_bytes=60 * 1024 * 1024
        ),
        name="fused",
    )(
        grad_out, dec_pre, ctrl_out, ctrl_mid, ctrl_in,
        dec_weight.reshape(9, C, C), zero_weight, ctrl_weight.reshape(9, C, C), *tabs,
    )

    grad_zero, grad_ctrl, grad_in = pl.pallas_call(
        finish,
        out_shape=[
            jax.ShapeDtypeStruct((20, 20), F32),
            jax.ShapeDtypeStruct((9, 20, 20), F32),
            jax.ShapeDtypeStruct((9, 20, 20), F32),
        ],
        in_specs=[vmem] * 3,
        out_specs=[vmem] * 3,
        name="finish",
    )(*blocks)
    return (grad_zero, grad_ctrl.reshape(3, 3, 20, 20), grad_in.reshape(3, 3, 20, 20))


def solution(mesh):
    tile = P("row", "col", None)
    return jax.shard_map(
        on_device,
        mesh=mesh,
        in_specs=(tile,) * 5 + (P(),) * 3,
        out_specs=(P("row", "col"), P(None, None, "row", "col"), P(None, None, "row", "col")),
        check_vma=False,
    )
```

time: 74.6 us -> 69.9 us (0.937)
  local copies, waits for them, and re-layouts: 4.25 us -> 0 us
    unnamed x3 -> x0, local copies, waits for them, and re-layouts: 2.26 us -> none
    slice x4 -> x0, local copies, waits for them, and re-layouts: 0.94 us -> none  [the longest x1 0.85 us: on_device(): both = jnp.concatenate([out_a[:, :30, :60], out_b[:, :30, :60]], axis=1)]
    transpose x1 -> x0, local copies, waits for them, and re-layouts: 0.83 us -> none  [on_device(): grad_zero = out_a[:, 30:40, :20].transpose(2, 0, 1).reshape(20, 20)]
    pallas_call x1 -> x2, Pallas kernels: 69.4 us -> 69.2 us  [the longest x1 66.5 us: on_device(): pl.pallas_call(kernel, out_shape=[jax.ShapeDtypeStruct((2, zn, 64), F32)...]
where the time goes in v2:
time: 69.9 us; the launch traced here: 69.8 us
  Pallas kernels  69.2 us (99%)
    pallas_call x1, Pallas kernels, on_device(): pl.pallas_call(kernel, out_shape=[jax.ShapeDtypeStruct((2, zn, 64), F32)...  66.5 us
    pallas_call x1, Pallas kernels, on_device(): pl.pallas_call(finish, out_shape=[jax.ShapeDtypeStruct((20, 20), F32), ja...  2.68 us

profile of v2, /device:TPU:1, one launch (start us, length us, event | category | flops | bytes accessed | tf_op | source)
XLA Modules:
  0.0 69.8 jit_solution(8878077437823572741)
XLA Ops:
  0.6 66.5 %fused.1 = (f32[2,48,64]{2,1,0:T(8,128)}, f32[2,32,64]{2,1,0:T(8,128)}, f32[2,16,64]{2,1,0:T(8,128)}) custom-call(bf16[32,32,320]{2,1,0:T(8,128)(2,1)} %g_hbm.1, bf16[32,32,320]{2,1,0:T(8,128)(2,1)} %pre_hbm.1, bf16[32,32,320]{2,1,0:T(8,128)(2,1)} %cout_hbm.1, bf16[32,32,320]{2,1,0:T(8,128)(2,1)} %mid_hbm.1, bf16[32,32,320]{2,1,0:T(8,128)(2,1)} %cin_hbm.1, ...), custom_call_target="tpu_custom_call" | custom-call | tf_op jit(solution)/shard_map/fused/pallas_call | solution.py:595
  67.1 2.7 %finish.1 = (f32[20,20]{1,0:T(8,128)}, f32[9,20,20]{2,1,0:T(8,128)}, f32[9,20,20]{2,1,0:T(8,128)}) custom-call(f32[2,48,64]{2,1,0:T(8,128)} %get-tuple-element.9.a_ref, f32[2,32,64]{2,1,0:T(8,128)} %get-tuple-element.10.b1_ref, f32[2,16,64]{2,1,0:T(8,128)} %get-tuple-element.11.b2_ref), custom_call_target="tpu_custom_call" | custom-call | tf_op jit(solution)/shard_map/finish/pallas_call | solution.py:646

commit v3 on v2

--- a/solution.py
+++ b/solution.py
@@ -13,8 +13,8 @@
 NN = (((1,), (0,)), ((), ()))
 C = 320
 T = 32
-ZA, ZB1, ZB2 = 48, 32, 16
-N_SEM = 80
+ZN, ZC = 32, 16
+N_SEM = 96
 
 
 def dot(a, b, dims=NN):
@@ -50,7 +50,7 @@
                 for i in range(10):
                     order[core * 160 + xl * 80 + z * 10 + i, 0] = (xl * 8 + z) * 20 + core * 10 + i
     deals = []
-    for zn, groups in ((ZA, 4), (ZB1, 2), (ZB2, 1)):
+    for zn, groups in ((ZN, 3), (ZC, 1)):
         deal = np.full((8 * zn, 1), -1, np.int32)
         for z in range(8):
             for g in range(groups):
@@ -62,9 +62,9 @@
 
 def kernel(
     g_hbm, pre_hbm, cout_hbm, mid_hbm, cin_hbm, wd_hbm, wz_hbm, wc_hbm,
-    place_hbm, order_hbm, deal_a_hbm, deal_b1_hbm, deal_b2_hbm,
-    out_a, out_b1, out_b2,
-    place_ref, order_ref, deal_a, deal_b1, deal_b2,
+    place_hbm, order_hbm, deal_hbm, deal_c_hbm,
+    out_a, out_b, out_c,
+    place_ref, order_ref, deal, deal_c,
     in4, pre, cout, wd, wz, wc,
     scol, hrow, hcol, hcor, hc32,
     shg, remg, shm, remm, shi, remi,
@@ -101,12 +101,10 @@
         pltpu.make_async_copy(cout_hbm, cout, load_sem.at[7]),
         pltpu.make_async_copy(order_hbm, order_ref, load_sem.at[8]),
         pltpu.make_async_copy(place_hbm, place_ref, load_sem.at[9]),
-        pltpu.make_async_copy(deal_a_hbm, deal_a, load_sem.at[10]),
-        pltpu.make_async_copy(deal_b1_hbm, deal_b1, load_sem.at[11]),
-        pltpu.make_async_copy(deal_b2_hbm, deal_b2, load_sem.at[12]),
+        pltpu.make_async_copy(deal_hbm, deal, load_sem.at[10]),
+        pltpu.make_async_copy(deal_c_hbm, deal_c, load_sem.at[11]),
     ]
-    for copy in loads:
-        copy.start()
+    loads[0].start()
 
     has = {-1: (row > 0, col > 0), 1: (row < 15, col < 15), 0: (row >= 0, col >= 0)}
     around = [(dr, dc) for dr in (-1, 0, 1) for dc in (-1, 0, 1) if (dr, dc) != (0, 0)]
@@ -129,6 +127,8 @@
         scol[1, n] = in4[n, :, T - 1, :]
 
     loads[0].wait()
+    for copy in loads[1:]:
+        copy.start()
     sides(0)
 
     count = jnp.int32(len(peers))
@@ -299,12 +299,10 @@
         )
 
     class Stage:
-        def __init__(self, out, deal, zn, sources, groups, rows, split, mine):
-            self.out, self.deal, self.zn, self.sources, self.groups = out, deal, zn, sources, groups
-            self.rows, self.split = rows, split
-            self.landings = mine[: len(sources)]
-            (self.d, self.ha, self.hb, self.pa, self.pb, self.e, self.f, self.ea, self.fb,
-             self.j, self.zs, self.zr, self.fin, self.pin) = mine[len(sources):]
+        def __init__(self, source, groups, rows, split, mine):
+            self.source, self.groups, self.rows, self.split = source, groups, rows, split
+            (self.landing, self.d, self.ha, self.hb, self.pa, self.pb,
+             self.e, self.f, self.ea, self.fb) = mine
             self.sent = []
 
         def go(self, *copies):
@@ -314,9 +312,7 @@
             return copies
 
         def one(self):
-            self.k1 = self.go(*[
-                remote(src.at[1 - core], dst, partner) for src, dst in zip(self.sources, self.landings)
-            ])
+            self.k1 = self.go(remote(self.source.at[1 - core], self.landing, partner))
 
         def put(self, base, yy, value):
             value = value.astype(BF16)
@@ -330,13 +326,13 @@
             for copy in self.k1:
                 copy.wait_recv()
 
-            def both(n, span, lanes):
-                here = self.sources[n][core, span, lanes].astype(F32)
-                return (here + self.landings[n][span, lanes].astype(F32)).astype(BF16)
+            def both(span, lanes):
+                here = self.source[core, span, lanes].astype(F32)
+                return (here + self.landing[span, lanes].astype(F32)).astype(BF16)
 
             for g in range(self.groups):
                 span = slice(g * 160, (g + 1) * 160)
-                parts = [both(0, span, slice(s * 256, (s + 1) * 256)) for s in range(4)]
+                parts = [both(span, slice(s * 256, (s + 1) * 256)) for s in range(4)]
                 for yy in range(4):
                     total = dot(parts[0], pmat[yy * 3])
                     for s in range(1, 3):
@@ -344,13 +340,13 @@
                     if yy == 3:
                         total += dot(parts[3], pmat[12])
                     self.put(g * 80, yy, total)
-            if len(self.sources) > 1:
-                main, last = (both(1, slice(0, 160), lanes) for lanes in (slice(0, 256), slice(256, 320)))
+            if self.groups == 0:
+                main, last = (both(slice(0, 160), lanes) for lanes in (slice(0, 256), slice(256, 320)))
                 for yy in range(4):
                     total = dot(main, pmat[yy * 3])
                     if yy == 3:
                         total += dot(last, pmat[12, 0:64])
-                    self.put(self.groups * 80, yy, total)
+                    self.put(0, yy, total)
 
             lo, hi = pl.ds(0, self.split), pl.ds(self.split, self.rows - self.split)
             far_y, far_x = (y + 2) % 4, (x + 2) % 4
@@ -398,19 +394,31 @@
                     remote(self.f.at[ty], self.fb.at[d - 1], at_y(ty)),
                 )
 
-        def four(self):
+        def collect(self, j, base):
             for copy in self.k4:
                 copy.wait_recv()
             total = self.e[x].astype(F32)
             for d in range(3):
                 total += self.ea[d].astype(F32)
-            self.j[0 : self.split] = total.astype(BF16)
+            j[base : base + self.split] = total.astype(BF16)
             total = self.f[y].astype(F32)
             for d in range(3):
                 total += self.fb[d].astype(F32)
-            self.j[self.split : self.rows] = total.astype(BF16)
+            j[base + self.split : base + self.rows] = total.astype(BF16)
+
+    class Last(Stage):
+        def __init__(self, out, table, zn, rows, parts, mine):
+            self.out, self.table, self.zn, self.rows, self.parts = out, table, zn, rows, parts
+            self.j, self.zs, self.zr, self.fin, self.pin = mine
+            self.sent = []
+
+        def four(self):
+            base = 0
+            for part in self.parts:
+                part.collect(self.j, base)
+                base += part.rows
             pick = jnp.where(
-                lax.broadcasted_iota(jnp.int32, (8 * self.zn, self.rows), 1) == self.deal[...], 1.0, 0.0
+                lax.broadcasted_iota(jnp.int32, (8 * self.zn, self.rows), 1) == self.table[...], 1.0, 0.0
             ).astype(BF16)
             self.zs[...] = dot(pick, self.j[...]).astype(BF16).reshape(8, self.zn, 128)
             self.k5 = []
@@ -435,9 +443,13 @@
             self.k6[0].wait_recv()
             self.show(1 - core, self.pin[...])
 
-    stage_a = Stage(out_a, deal_a, ZA, (ra, rz), 3, 320, 160, bufs[0:16])
-    stage_b1 = Stage(out_b1, deal_b1, ZB1, (rb1,), 2, 160, 80, bufs[16:31])
-    stage_b2 = Stage(out_b2, deal_b2, ZB2, (rb2,), 1, 80, 48, bufs[31:46])
+    stage_a = Stage(ra, 3, 240, 128, bufs[0:10])
+    stage_b1 = Stage(rb1, 2, 160, 80, bufs[10:20])
+    stage_b2 = Stage(rb2, 1, 80, 48, bufs[20:30])
+    stage_c = Stage(rz, 0, 80, 48, bufs[30:40])
+    last_a = Last(out_a, deal, ZN, 240, (stage_a,), bufs[40:45])
+    last_b = Last(out_b, deal, ZN, 240, (stage_b1, stage_b2), bufs[45:50])
+    last_c = Last(out_c, deal_c, ZC, 80, (stage_c,), bufs[50:55])
 
     loads[3].wait()
     arrange(wd, 0)
@@ -476,11 +488,8 @@
     turned(in4[3].reshape(1024, C))
     for a in range(3):
         weights(ra, a * 160, shm, remm, a)
-    loads[7].wait()
-    turned(dec)
-    halves(rz, 0, 0, C, dot(gt[...], cout[...].reshape(1024, C)))
     stage_a.one()
-    for n in range(9, 13):
+    for n in range(9, 12):
         loads[n].wait()
     depth = lax.broadcasted_iota(jnp.int32, (256, 256), 0)
 
@@ -521,28 +530,36 @@
     stage_a.three()
     stage_b1.two()
     stage_b2.two()
-    stage_a.four()
+    loads[7].wait()
+    turned(dec)
+    halves(rz, 0, 0, C, dot(gt[...], cout[...].reshape(1024, C)))
+    stage_c.one()
     stage_b1.relay()
     stage_b2.relay()
-    stage_a.five()
+    last_a.four()
+    stage_c.two()
     stage_b1.three()
     stage_b2.three()
-    stage_a.six()
-    stage_b1.four()
-    stage_b2.four()
-    stage_b1.five()
-    stage_b2.five()
-    stage_b1.six()
-    stage_b2.six()
+    stage_c.relay()
+    last_a.five()
+    last_b.four()
+    stage_c.three()
+    last_a.six()
+    last_c.four()
+    last_b.five()
+    last_b.six()
+    last_c.five()
+    last_c.six()
 
     for copies in (first, acts, second):
         for d, copy in copies:
             pl.when(there[d])(copy.wait_send)
-    for copy in stage_a.sent + stage_b1.sent + stage_b2.sent:
-        copy.wait_send()
-
-
-def finish(a_ref, b1_ref, b2_ref, zero_ref, ctrl_ref, in_ref):
+    for part in (stage_a, stage_b1, stage_b2, stage_c, last_a, last_b, last_c):
+        for copy in part.sent:
+            copy.wait_send()
+
+
+def finish(a_ref, b_ref, c_ref, zero_ref, ctrl_ref, in_ref):
     def exact(a, b, dims):
         return lax.dot_general(a, b, dims, precision=lax.Precision.HIGHEST, preferred_element_type=F32)
 
@@ -552,7 +569,7 @@
     for s in range(3):
         inside = (r >= s * 24) & (r < s * 24 + 20)
         sel = jnp.where(inside & (lane - s * 20 == r - s * 24), 1.0, sel)
-    for ref, groups, dst, base in ((a_ref, 4, ctrl_ref, 0), (b1_ref, 2, in_ref, 0), (b2_ref, 1, in_ref, 2)):
+    for ref, groups, dst in ((a_ref, 3, ctrl_ref), (b_ref, 3, in_ref), (c_ref, 1, None)):
         zn = ref.shape[1]
         turn = exact(sel, ref[...].reshape(2 * zn, 64), NT)
         k = lax.broadcasted_iota(jnp.int32, (2 * zn, 20), 0)
@@ -560,16 +577,17 @@
         for g in range(groups):
             pick = jnp.where(k == jnp.where(n < 10, n, n - 10 + zn) + g * 10, 1.0, 0.0)
             value = exact(turn, pick, NN)
-            if g == 3:
+            if dst is None:
                 zero_ref[...] = value[0:20]
             else:
                 for s in range(3):
-                    dst[(base + g) * 3 + s] = value[s * 24 : s * 24 + 20]
-
-
-def stage_buffers(landings, rows, split, zn):
+                    dst[g * 3 + s] = value[s * 24 : s * 24 + 20]
+
+
+def stage_buffers(landing, rows, split):
     rest = rows - split
-    return [pltpu.VMEM(shape, BF16) for shape in landings] + [
+    return [
+        pltpu.VMEM(landing, BF16),
         pltpu.VMEM((4, 4, rows, 128), BF16),
         pltpu.VMEM((2, 2, split, 128), BF16),
         pltpu.VMEM((2, 2, rest, 128), BF16),
@@ -579,6 +597,11 @@
         pltpu.VMEM((4, rest, 128), BF16),
         pltpu.VMEM((3, split, 128), BF16),
         pltpu.VMEM((3, rest, 128), BF16),
+    ]
+
+
+def last_buffers(rows, zn):
+    return [
         pltpu.VMEM((rows, 128), BF16),
         pltpu.VMEM((8, zn, 128), BF16),
         pltpu.VMEM((7, zn, 128), BF16),
@@ -594,8 +617,8 @@
     shifts = [pltpu.VMEM((3, T + 2, T, C), BF16), pltpu.VMEM((T + 2, T, 256), BF16)]
     blocks = pl.pallas_call(
         kernel,
-        out_shape=[jax.ShapeDtypeStruct((2, zn, 64), F32) for zn in (ZA, ZB1, ZB2)],
-        in_specs=[anys] * 13,
+        out_shape=[jax.ShapeDtypeStruct((2, zn, 64), F32) for zn in (ZN, ZN, ZC)],
+        in_specs=[anys] * 12,
         out_specs=[vmem] * 3,
         scratch_shapes=[
             *[pltpu.VMEM(t.shape, jnp.int32) for t in tabs],
@@ -624,11 +647,15 @@
             pltpu.VMEM((2, 320, 1024), BF16),
             pltpu.VMEM((2, 160, 1024), BF16),
         ]
-        + stage_buffers([(480, 1024), (160, C)], 320, 160, ZA)
-        + stage_buffers([(320, 1024)], 160, 80, ZB1)
-        + stage_buffers([(160, 1024)], 80, 48, ZB2)
+        + stage_buffers((480, 1024), 240, 128)
+        + stage_buffers((320, 1024), 160, 80)
+        + stage_buffers((160, 1024), 80, 48)
+        + stage_buffers((160, C), 80, 48)
+        + last_buffers(240, ZN)
+        + last_buffers(240, ZN)
+        + last_buffers(80, ZC)
         + [
-            pltpu.SemaphoreType.DMA((13,)),
+            pltpu.SemaphoreType.DMA((12,)),
             pltpu.SemaphoreType.DMA((3, 8)),
             pltpu.SemaphoreType.DMA((3, 8)),
             pltpu.SemaphoreType.DMA((N_SEM,)),

time: 69.9 us -> 71.2 us (1.019)
  Pallas kernels: 69.2 us -> 70.4 us
    pallas_call x1, Pallas kernels: 66.5 us -> 67.8 us  [on_device(): pl.pallas_call(kernel, out_shape=[jax.ShapeDtypeStruct((2, zn, 64), F32)...]
where the time goes in v3:
time: 71.2 us; the launch traced here: 71.1 us
  Pallas kernels  70.4 us (99%)
    pallas_call x1, Pallas kernels, on_device(): pl.pallas_call(kernel, out_shape=[jax.ShapeDtypeStruct((2, zn, 64), F32)...  67.8 us
    pallas_call x1, Pallas kernels, on_device(): pl.pallas_call(finish, out_shape=[jax.ShapeDtypeStruct((20, 20), F32), ja...  2.64 us

profile of v3, /device:TPU:1, one launch (start us, length us, event | category | flops | bytes accessed | tf_op | source)
XLA Modules:
  0.0 71.1 jit_solution(15154381215904125683)
XLA Ops:
  0.6 67.8 %fused.1 = (f32[2,32,64]{2,1,0:T(8,128)}, f32[2,32,64]{2,1,0:T(8,128)}, f32[2,16,64]{2,1,0:T(8,128)}) custom-call(bf16[32,32,320]{2,1,0:T(8,128)(2,1)} %g_hbm.1, bf16[32,32,320]{2,1,0:T(8,128)(2,1)} %pre_hbm.1, bf16[32,32,320]{2,1,0:T(8,128)(2,1)} %cout_hbm.1, bf16[32,32,320]{2,1,0:T(8,128)(2,1)} %mid_hbm.1, bf16[32,32,320]{2,1,0:T(8,128)(2,1)} %cin_hbm.1, ...), custom_call_target="tpu_custom_call" | custom-call | tf_op jit(solution)/shard_map/fused/pallas_call | solution.py:618
  68.4 2.6 %finish.1 = (f32[20,20]{1,0:T(8,128)}, f32[9,20,20]{2,1,0:T(8,128)}, f32[9,20,20]{2,1,0:T(8,128)}) custom-call(f32[2,32,64]{2,1,0:T(8,128)} %get-tuple-element.9.a_ref, f32[2,32,64]{2,1,0:T(8,128)} %get-tuple-element.10.b_ref, f32[2,16,64]{2,1,0:T(8,128)} %get-tuple-element.11.c_ref), custom_call_target="tpu_custom_call" | custom-call | tf_op jit(solution)/shard_map/finish/pallas_call | solution.py:673

commit v4 on v3

--- a/solution.py
+++ b/solution.py
@@ -68,7 +68,7 @@
     in4, pre, cout, wd, wz, wc,
     scol, hrow, hcol, hcor, hc32,
     shg, remg, shm, remm, shi, remi,
-    wrem, wn, tails, dec, pmat, omat, gt, mgrad,
+    wrem, wn, tails, acc, rate1, rate2, dec, pmat, omat, gt, mgrad,
     ra, rz, rb1, rb2,
     *rest,
 ):
@@ -122,6 +122,117 @@
     for peer in peers:
         pl.semaphore_signal(barrier, inc=1, device_id=peer, device_id_type=MESH)
 
+    edge = lax.broadcasted_iota(jnp.int32, (T, C), 0)
+    half_edge = lax.broadcasted_iota(jnp.int32, (16, C), 0)
+
+    def columns(k, act):
+        for side in range(2):
+            parts = (hcor[side, k].astype(F32), hcol[side, k].astype(F32), hcor[2 + side, k].astype(F32))
+            if act:
+                parts = [silu(v) for v in parts]
+            hc32[side, 0:1, :] = parts[0][15:16]
+            hc32[side, 1:33, :] = parts[1]
+            hc32[side, 33:34, :] = parts[2][0:1]
+
+    def emit(sh, i, cells, act, sides):
+        now = cells.astype(F32)
+        if act:
+            now = silu(now)
+        minus, plus = pltpu.roll(now, 1, 0), pltpu.roll(now, T - 1, 0)
+        if sides:
+            minus = jnp.where(edge == 0, hc32[0, pl.ds(i, 1), :], minus)
+            plus = jnp.where(edge == T - 1, hc32[1, pl.ds(i, 1), :], plus)
+        sh[0, i] = minus.astype(BF16)
+        sh[1, i] = now.astype(BF16)
+        sh[2, i] = plus.astype(BF16)
+
+    def inner(sh, k, act, sides):
+        @pl.loop(0, T, unroll=4)
+        def _(i):
+            emit(sh, i + 1, in4[k, i], act, sides)
+
+    def outer(sh, k, act):
+        emit(sh, 0, hrow[0, k], act, True)
+        emit(sh, T + 1, hrow[1, k], act, True)
+
+    def patch(sh):
+        @pl.loop(1, T + 1, unroll=4)
+        def _(i):
+            cells = sh[0, i, 0:16, :].astype(F32)
+            sh[0, i, 0:16, :] = jnp.where(half_edge == 0, hc32[0, pl.ds(i, 1), :], cells).astype(BF16)
+            cells = sh[2, i, 16:32, :].astype(F32)
+            sh[2, i, 16:32, :] = jnp.where(half_edge == 15, hc32[1, pl.ds(i, 1), :], cells).astype(BF16)
+
+    def gather_rem(sh, rem):
+        @pl.loop(0, 2)
+        def _(n):
+            span = pl.ds(n * 17, 17)
+            parts = [sh[k, span].reshape(544, C)[:, 256:320] for k in range(3)]
+            parts.append(jnp.zeros((544, 64), BF16))
+            rem[span] = jnp.concatenate(parts, axis=1).reshape(17, T, 256)
+
+    def arrange(w, slot):
+        for a in range(3):
+            for b in range(3):
+                wrem[slot, a, :, (2 - b) * 64 : (3 - b) * 64] = w[a * 3 + b, :, 256:320]
+                wn[slot, 2 - b, a * 64 : (a + 1) * 64, :] = w[a * 3 + b, 256:320, :256]
+            wrem[slot, a, :, 192:256] = jnp.zeros((C, 64), BF16)
+            wn[slot, 3, a * 64 : (a + 1) * 64, :] = wrem[slot, a, 256:320, :]
+        wn[slot, :, 192:256, :] = jnp.zeros((4, 64, 256), BF16)
+
+    def conv_tails(slot):
+        @pl.loop(0, 2)
+        def _(h):
+            span = pl.ds(h * 17, 17)
+            total = dot(remg[span].reshape(544, 256), wn[slot, 3], NT)
+            for s in range(3):
+                total += dot(shg[s, span].reshape(544, C)[:, :256], wn[slot, s], NT)
+            tails[span] = total.reshape(17, T, 256)
+
+    def conv(w, slot):
+        parts = []
+        for a in range(3):
+            span = pl.ds(2 - a, T)
+            for k in range(3):
+                parts.append((shg[k, span].reshape(1024, C)[:, :256], w[a * 3 + 2 - k, :256, :256]))
+            parts.append((remg[span].reshape(1024, 256), wrem[slot, a, :256, :]))
+        total = dot(*parts[0], NT)
+        for part in parts[1:]:
+            total += dot(*part, NT)
+        acc[...] = total
+
+    def scaled(dst, rate):
+        @pl.loop(0, 4)
+        def _(h):
+            span = pl.ds(h * 256, 256)
+            dst[span, 0:256] = (rate[span, 0:256] * acc[span, :]).astype(BF16)
+            last = (
+                tails[pl.ds(h * 8 + 2, 8)].reshape(256, 256)[:, :64]
+                + tails[pl.ds(h * 8 + 1, 8)].reshape(256, 256)[:, 64:128]
+                + tails[pl.ds(h * 8, 8)].reshape(256, 256)[:, 128:192]
+            )
+            dst[span, 256:320] = (rate[span, 256:320] * last).astype(BF16)
+
+    def slopes(dst, read):
+        @pl.loop(0, T, unroll=4)
+        def _(i):
+            dst[pl.ds(pl.multiple_of(i * T, T), T), :] = slope(read(i).astype(F32))
+
+    def turned(src):
+        for n in range(4):
+            gt[:, n * 256 : (n + 1) * 256] = dot(omat[...], src[n * 256 : (n + 1) * 256, :], NT).astype(BF16)
+
+    def halves(dst, base, lane, width, value):
+        value = value.astype(BF16)
+        for half in range(2):
+            dst[half, base : base + 160, lane : lane + width] = value[half * 160 : (half + 1) * 160]
+
+    def weights(dst, base, sh, rem, a):
+        span = pl.ds(a, T)
+        for s in range(3):
+            halves(dst, base, s * 256, 256, dot(gt[...], sh[s, span].reshape(1024, C)[:, :256]))
+        halves(dst, base, 768, 256, dot(gt[...], rem[span].reshape(1024, 256)))
+
     def sides(n):
         scol[0, n] = in4[n, :, 0, :]
         scol[1, n] = in4[n, :, T - 1, :]
@@ -130,6 +241,13 @@
     for copy in loads[1:]:
         copy.start()
     sides(0)
+
+    loads[1].wait()
+    loads[2].wait()
+    sides(1)
+    sides(2)
+    inner(shg, 0, False, False)
+    slopes(rate2, lambda i: in4[1, i])
 
     count = jnp.int32(len(peers))
     for d in around:
@@ -165,16 +283,16 @@
         for d, copy in copies:
             pl.when(there[d])(copy.start)
 
+    def finished(copies):
+        for d, copy in copies:
+            pl.when(there[d])(copy.wait_send)
+
     def landed(copies):
         for d, copy in copies:
             pl.when(there[(-d[0], -d[1])])(copy.wait_recv)
 
     first = halo(0, 1, 0)
     start(first)
-    loads[1].wait()
-    loads[2].wait()
-    sides(1)
-    sides(2)
     acts = halo(1, 2, 1)
     start(acts)
 
@@ -192,102 +310,6 @@
         edge_col = col == (0 if slot % 2 == 0 else 15)
         clear(jnp.logical_or(edge_row, edge_col), hcor, slot)
 
-    edge = lax.broadcasted_iota(jnp.int32, (T, C), 0)
-    half_edge = lax.broadcasted_iota(jnp.int32, (16, C), 0)
-
-    def columns(k, act):
-        for side in range(2):
-            parts = (hcor[side, k].astype(F32), hcol[side, k].astype(F32), hcor[2 + side, k].astype(F32))
-            if act:
-                parts = [silu(v) for v in parts]
-            hc32[side, 0:1, :] = parts[0][15:16]
-            hc32[side, 1:33, :] = parts[1]
-            hc32[side, 33:34, :] = parts[2][0:1]
-
-    def emit(sh, i, cells, act, sides):
-        now = cells.astype(F32)
-        if act:
-            now = silu(now)
-        minus, plus = pltpu.roll(now, 1, 0), pltpu.roll(now, T - 1, 0)
-        if sides:
-            minus = jnp.where(edge == 0, hc32[0, pl.ds(i, 1), :], minus)
-            plus = jnp.where(edge == T - 1, hc32[1, pl.ds(i, 1), :], plus)
-        sh[0, i] = minus.astype(BF16)
-        sh[1, i] = now.astype(BF16)
-        sh[2, i] = plus.astype(BF16)
-
-    def inner(sh, k, act, sides):
-        @pl.loop(0, T, unroll=4)
-        def _(i):
-            emit(sh, i + 1, in4[k, i], act, sides)
-
-    def outer(sh, k, act):
-        emit(sh, 0, hrow[0, k], act, True)
-        emit(sh, T + 1, hrow[1, k], act, True)
-
-    def patch(sh):
-        @pl.loop(1, T + 1, unroll=4)
-        def _(i):
-            cells = sh[0, i, 0:16, :].astype(F32)
-            sh[0, i, 0:16, :] = jnp.where(half_edge == 0, hc32[0, pl.ds(i, 1), :], cells).astype(BF16)
-            cells = sh[2, i, 16:32, :].astype(F32)
-            sh[2, i, 16:32, :] = jnp.where(half_edge == 15, hc32[1, pl.ds(i, 1), :], cells).astype(BF16)
-
-    def gather_rem(sh, rem):
-        @pl.loop(0, 2 * (T + 2) // 4)
-        def _(n):
-            span = pl.ds(n * 2, 2)
-            for s in range(3):
-                rem[span, :, s * 64 : (s + 1) * 64] = sh[s, span, :, 256:320]
-            rem[span, :, 192:256] = jnp.zeros((2, T, 64), BF16)
-
-    def arrange(w, slot):
-        for a in range(3):
-            for b in range(3):
-                wrem[slot, a, :, (2 - b) * 64 : (3 - b) * 64] = w[a * 3 + b, :, 256:320]
-                wn[slot, 2 - b, a * 64 : (a + 1) * 64, :] = w[a * 3 + b, 256:320, :256]
-            wrem[slot, a, :, 192:256] = jnp.zeros((C, 64), BF16)
-            wn[slot, 3, a * 64 : (a + 1) * 64, :] = wrem[slot, a, 256:320, :]
-        wn[slot, :, 192:256, :] = jnp.zeros((4, 64, 256), BF16)
-
-    def conv_tails(slot):
-        @pl.loop(0, 2)
-        def _(h):
-            span = pl.ds(h * 17, 17)
-            total = dot(remg[span].reshape(544, 256), wn[slot, 3], NT)
-            for s in range(3):
-                total += dot(shg[s, span].reshape(544, C)[:, :256], wn[slot, s], NT)
-            tails[span] = total.reshape(17, T, 256)
-
-    def conv(w, slot, i0):
-        total = jnp.zeros((512, 256), F32)
-        for a in range(3):
-            span = pl.ds(i0 + 2 - a, 16)
-            for s in range(3):
-                total += dot(shg[s, span].reshape(512, C)[:, :256], w[a * 3 + 2 - s, :256, :256], NT)
-            total += dot(remg[span].reshape(512, 256), wrem[slot, a, :256, :], NT)
-        last = (
-            tails[pl.ds(i0 + 2, 16)].reshape(512, 256)[:, :64]
-            + tails[pl.ds(i0 + 1, 16)].reshape(512, 256)[:, 64:128]
-            + tails[pl.ds(i0, 16)].reshape(512, 256)[:, 128:192]
-        )
-        return total, last
-
-    def turned(src):
-        for n in range(4):
-            gt[:, n * 256 : (n + 1) * 256] = dot(omat[...], src[n * 256 : (n + 1) * 256, :], NT).astype(BF16)
-
-    def halves(dst, base, lane, width, value):
-        value = value.astype(BF16)
-        for half in range(2):
-            dst[half, base : base + 160, lane : lane + width] = value[half * 160 : (half + 1) * 160]
-
-    def weights(dst, base, sh, rem, a):
-        span = pl.ds(a, T)
-        for s in range(3):
-            halves(dst, base, s * 256, 256, dot(gt[...], sh[s, span].reshape(1024, C)[:, :256]))
-        halves(dst, base, 768, 256, dot(gt[...], rem[span].reshape(1024, 256)))
-
     counter = [0]
 
     def remote(src, dst, peer):
@@ -310,6 +332,11 @@
                 copy.start()
             self.sent += copies
             return copies
+
+        def drain(self):
+            for copy in self.sent:
+                copy.wait_send()
+            self.sent = []
 
         def one(self):
             self.k1 = self.go(remote(self.source.at[1 - core], self.landing, partner))
@@ -453,33 +480,36 @@
 
     loads[3].wait()
     arrange(wd, 0)
-    inner(shg, 0, False, False)
+    loads[4].wait()
+    slopes(rate1, lambda i: pre[i])
+    loads[8].wait()
+    omat[...] = jnp.where(
+        lax.broadcasted_iota(jnp.int32, (C, C), 1) == order_ref[...], 1.0, 0.0
+    ).astype(BF16)
+    for n in range(9, 12):
+        loads[n].wait()
+    depth = lax.broadcasted_iota(jnp.int32, (256, 256), 0)
+
+    @pl.loop(0, 13)
+    def _(k):
+        pmat[k] = jnp.where(depth == place_ref[pl.ds(k, 1), :], 1.0, 0.0).astype(BF16)
+
+    loads[6].wait()
+    arrange(wc, 1)
     landed(first)
     columns(0, False)
     outer(shg, 0, False)
     patch(shg)
     gather_rem(shg, remg)
-    loads[4].wait()
+    conv_tails(0)
+    conv(wd, 0)
+    scaled(dec, rate1)
     loads[5].wait()
-    conv_tails(0)
-
-    @pl.loop(0, 2)
-    def _(h):
-        main, last = conv(wd, 0, h * 16)
-        rate = slope(pre[pl.ds(h * 16, 16)].reshape(512, C).astype(F32))
-        dec[pl.ds(h * 512, 512), 0:256] = (rate[:, :256] * main).astype(BF16)
-        dec[pl.ds(h * 512, 512), 256:320] = (rate[:, 256:] * last).astype(BF16)
-        grad = dec[pl.ds(h * 512, 512), :]
-        in4[3, pl.ds(h * 16, 16)] = dot(grad, wz[...], NT).astype(BF16).reshape(16, T, C)
-
+    in4[3] = dot(dec[...], wz[...], NT).astype(BF16).reshape(T, T, C)
     sides(3)
     second = halo(3, 1, 2)
     start(second)
 
-    loads[8].wait()
-    omat[...] = jnp.where(
-        lax.broadcasted_iota(jnp.int32, (C, C), 1) == order_ref[...], 1.0, 0.0
-    ).astype(BF16)
     landed(acts)
     columns(1, True)
     inner(shm, 1, True, True)
@@ -489,16 +519,10 @@
     for a in range(3):
         weights(ra, a * 160, shm, remm, a)
     stage_a.one()
-    for n in range(9, 12):
-        loads[n].wait()
-    depth = lax.broadcasted_iota(jnp.int32, (256, 256), 0)
-
-    @pl.loop(0, 13)
-    def _(k):
-        pmat[k] = jnp.where(depth == place_ref[pl.ds(k, 1), :], 1.0, 0.0).astype(BF16)
-
-    loads[6].wait()
-    arrange(wc, 1)
+    loads[7].wait()
+    turned(dec)
+    halves(rz, 0, 0, C, dot(gt[...], cout[...].reshape(1024, C)))
+    stage_c.one()
     inner(shg, 3, False, False)
     landed(second)
     columns(3, False)
@@ -506,57 +530,45 @@
     patch(shg)
     gather_rem(shg, remg)
     stage_a.two()
+    stage_c.two()
     columns(2, True)
     inner(shi, 2, True, True)
     outer(shi, 2, True)
     gather_rem(shi, remi)
     conv_tails(1)
-
-    def second_half(h):
-        main, last = conv(wc, 1, h * 16)
-        rate = slope(in4[1, h * 16 : (h + 1) * 16].reshape(512, C).astype(F32))
-        mgrad[h * 512 : (h + 1) * 512, 0:256] = (rate[:, :256] * main).astype(BF16)
-        mgrad[h * 512 : (h + 1) * 512, 256:320] = (rate[:, 256:] * last).astype(BF16)
-
-    second_half(0)
+    conv(wc, 1)
     stage_a.relay()
-    second_half(1)
+    stage_c.relay()
+    scaled(mgrad, rate2)
     turned(mgrad)
     for a in range(2):
         weights(rb1, a * 160, shi, remi, a)
     stage_b1.one()
     weights(rb2, 0, shi, remi, 2)
     stage_b2.one()
-    stage_a.three()
     stage_b1.two()
     stage_b2.two()
-    loads[7].wait()
-    turned(dec)
-    halves(rz, 0, 0, C, dot(gt[...], cout[...].reshape(1024, C)))
-    stage_c.one()
+    stage_a.three()
+    stage_c.three()
     stage_b1.relay()
     stage_b2.relay()
     last_a.four()
-    stage_c.two()
+    last_c.four()
     stage_b1.three()
     stage_b2.three()
-    stage_c.relay()
+    last_b.four()
     last_a.five()
-    last_b.four()
-    stage_c.three()
+    last_c.five()
     last_a.six()
-    last_c.four()
+    last_c.six()
+    finished(first)
+    finished(acts)
+    finished(second)
+    for part in (stage_a, stage_b1, stage_b2, stage_c, last_a, last_b, last_c):
+        part.drain()
     last_b.five()
     last_b.six()
-    last_c.five()
-    last_c.six()
-
-    for copies in (first, acts, second):
-        for d, copy in copies:
-            pl.when(there[d])(copy.wait_send)
-    for part in (stage_a, stage_b1, stage_b2, stage_c, last_a, last_b, last_c):
-        for copy in part.sent:
-            copy.wait_send()
+    last_b.drain()
 
 
 def finish(a_ref, b_ref, c_ref, zero_ref, ctrl_ref, in_ref):
@@ -637,6 +649,9 @@
             pltpu.VMEM((2, 3, C, 256), BF16),
             pltpu.VMEM((2, 4, 256, 256), BF16),
             pltpu.VMEM((T + 2, T, 256), F32),
+            pltpu.VMEM((1024, 256), F32),
+            pltpu.VMEM((1024, C), F32),
+            pltpu.VMEM((1024, C), F32),
             pltpu.VMEM((1024, C), BF16),
             pltpu.VMEM((13, 256, 256), BF16),
             pltpu.VMEM((C, C), BF16),

time: 71.2 us -> 68.2 us (0.958)
  Pallas kernels: 70.4 us -> 67.4 us
    pallas_call x1, Pallas kernels: 67.8 us -> 64.7 us  [on_device(): pl.pallas_call(kernel, out_shape=[jax.ShapeDtypeStruct((2, zn, 64), F32)...]
where the time goes in v4:
time: 68.2 us; the launch traced here: 68 us
  Pallas kernels  67.4 us (99%)
    pallas_call x1, Pallas kernels, on_device(): pl.pallas_call(kernel, out_shape=[jax.ShapeDtypeStruct((2, zn, 64), F32)...  64.7 us
    pallas_call x1, Pallas kernels, on_device(): pl.pallas_call(finish, out_shape=[jax.ShapeDtypeStruct((20, 20), F32), ja...  2.64 us

profile of v4, /device:TPU:1, one launch (start us, length us, event | category | flops | bytes accessed | tf_op | source)
XLA Modules:
  0.0 68.0 jit_solution(8147933616212451549)
XLA Ops:
  0.6 64.7 %fused.1 = (f32[2,32,64]{2,1,0:T(8,128)}, f32[2,32,64]{2,1,0:T(8,128)}, f32[2,16,64]{2,1,0:T(8,128)}) custom-call(bf16[32,32,320]{2,1,0:T(8,128)(2,1)} %g_hbm.1, bf16[32,32,320]{2,1,0:T(8,128)(2,1)} %pre_hbm.1, bf16[32,32,320]{2,1,0:T(8,128)(2,1)} %cout_hbm.1, bf16[32,32,320]{2,1,0:T(8,128)(2,1)} %mid_hbm.1, bf16[32,32,320]{2,1,0:T(8,128)(2,1)} %cin_hbm.1, ...), custom_call_target="tpu_custom_call" | custom-call | tf_op jit(solution)/shard_map/fused/pallas_call | solution.py:630
  65.4 2.6 %finish.1 = (f32[20,20]{1,0:T(8,128)}, f32[9,20,20]{2,1,0:T(8,128)}, f32[9,20,20]{2,1,0:T(8,128)}) custom-call(f32[2,32,64]{2,1,0:T(8,128)} %get-tuple-element.9.a_ref, f32[2,32,64]{2,1,0:T(8,128)} %get-tuple-element.10.b_ref, f32[2,16,64]{2,1,0:T(8,128)} %get-tuple-element.11.c_ref), custom_call_target="tpu_custom_call" | custom-call | tf_op jit(solution)/shard_map/finish/pallas_call | solution.py:688

commit v5 on v4

--- a/solution.py
+++ b/solution.py
@@ -69,7 +69,7 @@
     scol, hrow, hcol, hcor, hc32,
     shg, remg, shm, remm, shi, remi,
     wrem, wn, tails, acc, rate1, rate2, dec, pmat, omat, gt, mgrad,
-    ra, rz, rb1, rb2,
+    ra, rz, rb1, rb2, picks, picks_c,
     *rest,
 ):
     bufs, (load_sem, hs_sem, hr_sem, send_sem, recv_sem) = rest[:-5], rest[-5:]
@@ -434,8 +434,8 @@
             j[base + self.split : base + self.rows] = total.astype(BF16)
 
     class Last(Stage):
-        def __init__(self, out, table, zn, rows, parts, mine):
-            self.out, self.table, self.zn, self.rows, self.parts = out, table, zn, rows, parts
+        def __init__(self, out, pick, zn, parts, mine):
+            self.out, self.pick, self.zn, self.parts = out, pick, zn, parts
             self.j, self.zs, self.zr, self.fin, self.pin = mine
             self.sent = []
 
@@ -444,10 +444,7 @@
             for part in self.parts:
                 part.collect(self.j, base)
                 base += part.rows
-            pick = jnp.where(
-                lax.broadcasted_iota(jnp.int32, (8 * self.zn, self.rows), 1) == self.table[...], 1.0, 0.0
-            ).astype(BF16)
-            self.zs[...] = dot(pick, self.j[...]).astype(BF16).reshape(8, self.zn, 128)
+            self.zs[...] = dot(self.pick[...], self.j[...]).astype(BF16).reshape(8, self.zn, 128)
             self.k5 = []
             for d in (4, 3, 5, 2, 6, 1, 7):
                 tz = (z + d) % 8
@@ -474,9 +471,9 @@
     stage_b1 = Stage(rb1, 2, 160, 80, bufs[10:20])
     stage_b2 = Stage(rb2, 1, 80, 48, bufs[20:30])
     stage_c = Stage(rz, 0, 80, 48, bufs[30:40])
-    last_a = Last(out_a, deal, ZN, 240, (stage_a,), bufs[40:45])
-    last_b = Last(out_b, deal, ZN, 240, (stage_b1, stage_b2), bufs[45:50])
-    last_c = Last(out_c, deal_c, ZC, 80, (stage_c,), bufs[50:55])
+    last_a = Last(out_a, picks, ZN, (stage_a,), bufs[40:45])
+    last_b = Last(out_b, picks, ZN, (stage_b1, stage_b2), bufs[45:50])
+    last_c = Last(out_c, picks_c, ZC, (stage_c,), bufs[50:55])
 
     loads[3].wait()
     arrange(wd, 0)
@@ -496,6 +493,12 @@
 
     loads[6].wait()
     arrange(wc, 1)
+    inner(shm, 1, True, False)
+    inner(shi, 2, True, False)
+    for pick, table in ((picks, deal), (picks_c, deal_c)):
+        pick[...] = jnp.where(
+            lax.broadcasted_iota(jnp.int32, pick.shape, 1) == table[...], 1.0, 0.0
+        ).astype(BF16)
     landed(first)
     columns(0, False)
     outer(shg, 0, False)
@@ -512,8 +515,8 @@
 
     landed(acts)
     columns(1, True)
-    inner(shm, 1, True, True)
     outer(shm, 1, True)
+    patch(shm)
     gather_rem(shm, remm)
     turned(in4[3].reshape(1024, C))
     for a in range(3):
@@ -532,8 +535,8 @@
     stage_a.two()
     stage_c.two()
     columns(2, True)
-    inner(shi, 2, True, True)
     outer(shi, 2, True)
+    patch(shi)
     gather_rem(shi, remi)
     conv_tails(1)
     conv(wc, 1)
@@ -661,6 +664,8 @@
             pltpu.VMEM((2, 160, C), BF16),
             pltpu.VMEM((2, 320, 1024), BF16),
             pltpu.VMEM((2, 160, 1024), BF16),
+            pltpu.VMEM((8 * ZN, 240), BF16),
+            pltpu.VMEM((8 * ZC, 80), BF16),
         ]
         + stage_buffers((480, 1024), 240, 128)
         + stage_buffers((320, 1024), 160, 80)

time: 68.2 us -> 67.4 us (0.988)
  Pallas kernels: 67.4 us -> 66.6 us
    pallas_call x1, Pallas kernels: 64.7 us -> 64 us  [on_device(): pl.pallas_call(kernel, out_shape=[jax.ShapeDtypeStruct((2, zn, 64), F32)...]
where the time goes in v5:
time: 67.4 us; the launch traced here: 67.3 us
  Pallas kernels  66.6 us (99%)
    pallas_call x1, Pallas kernels, on_device(): pl.pallas_call(kernel, out_shape=[jax.ShapeDtypeStruct((2, zn, 64), F32)...  64 us
    pallas_call x1, Pallas kernels, on_device(): pl.pallas_call(finish, out_shape=[jax.ShapeDtypeStruct((20, 20), F32), ja...  2.64 us

profile of v5, /device:TPU:1, one launch (start us, length us, event | category | flops | bytes accessed | tf_op | source)
XLA Modules:
  0.0 67.3 jit_solution(4665885792715219331)
XLA Ops:
  0.6 64.0 %fused.1 = (f32[2,32,64]{2,1,0:T(8,128)}, f32[2,32,64]{2,1,0:T(8,128)}, f32[2,16,64]{2,1,0:T(8,128)}) custom-call(bf16[32,32,320]{2,1,0:T(8,128)(2,1)} %g_hbm.1, bf16[32,32,320]{2,1,0:T(8,128)(2,1)} %pre_hbm.1, bf16[32,32,320]{2,1,0:T(8,128)(2,1)} %cout_hbm.1, bf16[32,32,320]{2,1,0:T(8,128)(2,1)} %mid_hbm.1, bf16[32,32,320]{2,1,0:T(8,128)(2,1)} %cin_hbm.1, ...), custom_call_target="tpu_custom_call" | custom-call | tf_op jit(solution)/shard_map/fused/pallas_call | solution.py:633
  64.6 2.6 %finish.1 = (f32[20,20]{1,0:T(8,128)}, f32[9,20,20]{2,1,0:T(8,128)}, f32[9,20,20]{2,1,0:T(8,128)}) custom-call(f32[2,32,64]{2,1,0:T(8,128)} %get-tuple-element.9.a_ref, f32[2,32,64]{2,1,0:T(8,128)} %get-tuple-element.10.b_ref, f32[2,16,64]{2,1,0:T(8,128)} %get-tuple-element.11.c_ref), custom_call_target="tpu_custom_call" | custom-call | tf_op jit(solution)/shard_map/finish/pallas_call | solution.py:693
